TPU v7x, 256 devices: a whole 4x4x8 slice. The times are simulated.
256 devices in a mesh: hst: 16 (over z, core), local: 16 (over y, x).
Axes of the slice: x: 4, y: 4, z: 8, core: 2. Of those that a mesh axis runs over, the one named last changes fastest.
Arguments:
- teacher_logits: bfloat16 [512, 24, 32000], P(('hst', 'local')), may hold values from -360 to 450
- sample_ids: int32 [512, 24], P(('hst', 'local')), may hold values from 0 to 23, as said below
- client_counts: int32 [512], P(('hst', 'local')), may hold values from 1 to 999
- student_hidden: bfloat16 [24, 4096], replicated, may hold values from -60 to 60
- student_weight: bfloat16 [4096, 32000], P(None, ('hst', 'local')), may hold values from -0.0625 to 0.0625
Outputs:
- grad_weight: bfloat16 [4096, 32000], P(None, ('hst', 'local'))
- grad_hidden: float32 [24, 4096], P(None, ('hst', 'local'))
Inputs may be any that keep to these rules, and one draw needn't show every extreme that they name: `sample_ids`: for each client the row is a permutation of 0 to 23.
All inputs are finite; a program needn't handle non-finite values.
Results may differ from a plain program's by a relative error of at most 0.0056.
Values sent between devices are 32-bit elements; how exact they have to be, the bound alone decides.
A program may use at most 64 MiB of HBM per device.

v0:
```python
import jax
import jax.numpy as jnp
from jax import lax
from jax.sharding import Mesh
from jax.sharding import PartitionSpec as P

HST_LOCAL = ("hst_0", "hst_1", "local_0", "local_1")


def sent_to_all(shard, axis):
    devices = lax.axis_size(axis)
    return lax.all_to_all(
        jnp.broadcast_to(shard[None], (devices, *shard.shape)), axis, 0, 0, tiled=True
    )


def over_copies(shard, axis):
    everything = sent_to_all(shard, axis)
    return jnp.sum(everything, axis=0)


def one_axis_at_a_time(shard, axes):
    far, near = axes
    return over_copies(over_copies(shard, near), far)


def cut_along(shard, dim, devices):
    lengths = shard.shape
    blocks = shard.reshape(*lengths[:dim], devices, lengths[dim] // devices, *lengths[dim + 1 :])
    return jnp.moveaxis(blocks, dim, 0)


def sum_at_owner(shard, axis, dim):
    blocks = cut_along(shard, dim, lax.axis_size(axis))
    arrived = lax.all_to_all(blocks, axis, split_axis=0, concat_axis=0, tiled=True)
    return arrived.sum(axis=0)


def sum_in_two_steps(shard, axes, dim):
    far, near = axes
    own = sum_at_owner(cut_along(shard, dim, lax.axis_size(far)), near, dim + 1)
    return jnp.sum(lax.all_to_all(own, far, 0, 0, tiled=True), axis=0)


def gathered_once(shard, axis):
    leaves = jax.tree.leaves(shard)
    turns = sorted(range(len(leaves)), key=lambda k: -leaves[k].size)
    width = (1, *leaves[turns[0]].shape)[-1]
    lines = [
        jnp.pad(leaves[k].reshape(-1), (0, -leaves[k].size % width)).reshape(-1, width)
        for k in turns
    ]
    both, at, found = (lax.all_gather(jnp.concatenate(lines), axis), 0, {})
    for k, line in zip(turns, lines):
        section = both[:, at : at + len(line)].reshape(len(both), -1)
        found[k] = section[:, : leaves[k].size].reshape(-1, *leaves[k].shape)
        at += len(line)
    numbers = iter(range(len(leaves)))
    return jax.tree.map(lambda _: found[next(numbers)], shard)


def joined_all(shard, axes, combine):
    for axis in axes:
        pieces = gathered_once(shard, axis)
        shard = jax.tree.map(lambda part: part[0], pieces)
        for k in range(1, lax.axis_size(axis)):
            shard = combine(shard, jax.tree.map(lambda part: part[k], pieces))
    return shard


def combine_pair(first, second):
    first_max, first_total = first
    second_max, second_total = second
    joined = jnp.maximum(first_max, second_max)
    return (
        joined,
        first_total * jnp.exp(first_max - joined) + second_total * jnp.exp(second_max - joined),
    )


def combine_four(first, second):
    teacher = combine_pair((first[0], first[1]), (second[0], second[1]))
    student = combine_pair((first[2], first[3]), (second[2], second[3]))
    return (teacher[0], teacher[1], student[0], student[1])


def local_stats(values):
    row_max = jnp.max(values, axis=1)
    row_total = jnp.sum(jnp.exp(values - row_max[:, None]), axis=1)
    return (row_max, row_total)


def per_device(teacher_logits, sample_ids, client_counts, student_hidden, student_weight):
    samples = teacher_logits.shape[1]
    client_weight = client_counts.astype(jnp.float32)
    count_total = one_axis_at_a_time(
        jnp.sum(client_weight), (("hst_0", "hst_1", "local_0"), "local_1")
    )
    places = jnp.arange(samples, dtype=jnp.int32)
    weighted = jnp.zeros((samples, teacher_logits.shape[2]), jnp.float32)
    for client in range(teacher_logits.shape[0]):
        selector = (sample_ids[client][None, :] == places[:, None]).astype(jnp.bfloat16)
        aligned = jnp.dot(selector, teacher_logits[client], preferred_element_type=jnp.float32)
        weighted = weighted + client_weight[client] * aligned
    student_logits = jnp.dot(student_hidden, student_weight, preferred_element_type=jnp.float32)
    student_max, student_total = local_stats(student_logits)
    summed = sum_in_two_steps(weighted, (("hst_0", "hst_1", "local_0"), "local_1"), 1)
    ensemble = summed / count_total
    teacher_max, teacher_total = local_stats(ensemble)
    teacher_max, teacher_total, student_max, student_total = joined_all(
        (teacher_max, teacher_total, student_max, student_total), HST_LOCAL, combine_four
    )
    teacher_prob = jnp.exp(ensemble - teacher_max[:, None]) / teacher_total[:, None]
    student_prob = jnp.exp(student_logits - student_max[:, None]) / student_total[:, None]
    grad_logits = (32768.0 / samples * (student_prob - teacher_prob)).astype(jnp.bfloat16)
    grad_weight = jnp.dot(student_hidden.T, grad_logits, preferred_element_type=jnp.float32).astype(
        jnp.bfloat16
    )
    partial_value = lax.dot_general(
        grad_logits, student_weight, (((1,), (1,)), ((), ())), preferred_element_type=jnp.float32
    )
    grad_hidden = sum_in_two_steps(partial_value, (("hst_0", "hst_1", "local_0"), "local_1"), 1)
    return (grad_weight, grad_hidden)


def solution(mesh):
    finer = Mesh(mesh.devices.reshape(8, 2, 4, 4), ("hst_0", "hst_1", "local_0", "local_1"))
    return jax.shard_map(
        per_device,
        mesh=finer,
        in_specs=(
            P(HST_LOCAL, None, None),
            P(HST_LOCAL, None),
            P(HST_LOCAL),
            P(),
            P(None, HST_LOCAL),
        ),
        out_specs=(P(None, HST_LOCAL), P(None, HST_LOCAL)),
        check_vma=False,
    )
```

profile of v0, /device:TPU:1, one launch (start us, length us, event | category | flops | bytes accessed | tf_op | source)
XLA Modules:
  0.0 213.0 jit_solution(2647974430486995060)
XLA Ops:
  0.6 1.3 convert_reduce_fusion
  2.0 1.2 broadcast_in_dim.4
  3.2 4.8 %all-to-all-start.2 = ((f32[4,1,1]{2,1,0:T(1,128)}), f32[4,1,1]{2,1,0:T(1,128)S(1)}, u32[]{:S(2)}, u32[]{:S(2)}) async-start(f32[4,1,1]{2,1,0:T(1,128)} %broadcast_in_dim.4), calls=%async_computation.2 | async-start | bytes 4096 | tf_op jit(solution)/shard_map/all_to_all | solution.py:12
  8.1 0.8 convert_element_type.14
  8.9 0.7 fusion.130
  9.5 0.8 slice_bitcast_fusion.73
  10.3 2.6 %convolution_multiply_fusion = f32[24,32000]{1,0:T(8,128)S(1)} fusion(bf16[2,24,32000]{2,1,0:T(8,128)(2,1)} %param.5, f32[]{:T(128)} %bitcast.3, s32[24]{0:T(128)S(1)} %get-tuple-element.39), kind=kOutput, calls=%fused_computation | convolution fusion | flops 37632576 | bytes 4608608 | tf_op jit(solution)/shard_map/dot_general | solution.py:103
  12.9 3.0 %fusion = f32[24,32000]{1,0:T(8,128)} fusion(f32[24,32000]{1,0:T(8,128)S(1)} %convolution_multiply_fusion, bf16[2,24,32000]{2,1,0:T(8,128)(2,1)S(1)} %copy-done.1, f32[]{:T(128)} %bitcast, s32[24]{0:T(128)S(1)} %get-tuple-element.38), kind=kOutput, calls=%fused_computation.2 | convolution fusion | flops 38400576 | bytes 7680516 | tf_op jit(solution)/shard_map/dot_general | solution.py:103
  15.9 5.5 %reshape.1568 = f32[24,64,500]{2,1,0:T(8,128)} reshape(f32[24,32000]{1,0:T(8,128)} %fusion) | data formatting | bytes 6144000 | tf_op jit(solution)/shard_map/reshape | solution.py:29
  21.4 5.4 %copy.59 = f32[24,64,500]{2,0,1:T(8,128)} copy(f32[24,64,500]{2,1,0:T(8,128)} %reshape.1568) | data formatting | bytes 6144000 | tf_op jit(solution)/shard_map/reshape | solution.py:29
  26.8 5.2 %reshape.1569 = f32[64,24,4,125]{3,2,1,0:T(4,128)} reshape(f32[64,24,500]{2,1,0:T(8,128)} %bitcast.699) | data formatting | bytes 6144000 | tf_op jit(solution)/shard_map/reshape | solution.py:29
  32.0 5.4 %copy.43 = f32[4,64,24,125]{3,1,2,0:T(8,128)} copy(f32[4,64,24,125]{3,0,2,1:T(4,128)} %bitcast.700) | data formatting | bytes 6144000 | tf_op jit(solution)/shard_map/transpose | solution.py:30
  37.4 4.6 %all-to-all-start = ((f32[4,64,24,125]{3,1,2,0:T(8,128)}), f32[4,64,24,125]{3,1,2,0:T(8,128)}, u32[]{:S(2)}, u32[]{:S(2)}) async-start(f32[4,64,24,125]{3,1,2,0:T(8,128)} %copy.43), calls=%async_computation | async-start | bytes 6291456 | tf_op jit(solution)/shard_map/all_to_all | solution.py:35
  42.1 0.6 reduce_sum.84
  42.7 35.4 %all-to-all-done = f32[4,64,24,125]{3,1,2,0:T(8,128)} async-done(((f32[4,64,24,125]{3,1,2,0:T(8,128)}), f32[4,64,24,125]{3,1,2,0:T(8,128)}, u32[]{:S(2)}, u32[]{:S(2)}) %all-to-all-start) | async-done | bytes 3072032 | tf_op jit(solution)/shard_map/all_to_all | solution.py:35
  78.0 1.3 broadcast_in_dim.5
  79.3 14.3 %all-to-all-start.3 = ((f32[64,1,1]{2,1,0:T(1,128)}), f32[64,1,1]{2,1,0:T(1,128)S(1)}, u32[]{:S(2)}, u32[]{:S(2)}) async-start(f32[64,1,1]{2,1,0:T(1,128)} %broadcast_in_dim.5), calls=%async_computation.3 | async-start | bytes 65536 | tf_op jit(solution)/shard_map/all_to_all | solution.py:12
  93.6 2.4 %reduce_sum.81 = f32[64,24,125]{2,0,1:T(8,128)S(1)} reduce(f32[4,64,24,125]{3,1,2,0:T(8,128)} %all-to-all-done, f32[]{:T(128)} %constant.3.clone.1), dimensions={0}, to_apply=%region_0.0 | reduce | flops 576000 | bytes 3840004 | tf_op jit(solution)/shard_map/reduce_sum | solution.py:36
  96.0 1.3 copy.45
  97.3 5.5 %all-to-all-done.3 = f32[64,1,1]{2,1,0:T(1,128)S(1)} async-done(((f32[64,1,1]{2,1,0:T(1,128)}), f32[64,1,1]{2,1,0:T(1,128)S(1)}, u32[]{:S(2)}, u32[]{:S(2)}) %all-to-all-start.3) | async-done | bytes 288 | tf_op jit(solution)/shard_map/all_to_all | solution.py:12
  102.8 5.0 %all-to-all-start.1 = ((f32[64,24,125]{2,1,0:T(8,128)}), f32[64,24,125]{2,1,0:T(8,128)S(1)}, u32[]{:S(2)}, u32[]{:S(2)}) async-start(f32[64,24,125]{2,1,0:T(8,128)} %copy.45), calls=%async_computation.1 | async-start | bytes 1572864 | tf_op jit(solution)/shard_map/all_to_all | solution.py:42
  107.8 0.4 fusion.131
  108.2 0.2 exponential_reduce_fusion
  108.4 0.7 reduce_sum.85
  109.1 21.5 %all-to-all-done.1 = f32[64,24,125]{2,1,0:T(8,128)S(1)} async-done(((f32[64,24,125]{2,1,0:T(8,128)}), f32[64,24,125]{2,1,0:T(8,128)S(1)}, u32[]{:S(2)}, u32[]{:S(2)}) %all-to-all-start.1) | async-done | bytes 768032 | tf_op jit(solution)/shard_map/all_to_all | solution.py:42
  130.7 0.8 fusion.120
  131.5 0.8 exponential_reduce_fusion.1
  132.3 15.6 %all-gather.4 = f32[8,4,24]{2,1,0:T(4,128)S(1)} all-gather(f32[1,4,24]{2,1,0:T(4,128)S(1)} %maximum_bitcast_fusion), channel_id=2, replica_groups=mesh['hst_0'=8,'hst_1'=2,'local_0'=4,'local_1'=4] {'hst_0'}, dimensions={0}, use_global_device_ids=true | all-gather | bytes 3456 | tf_op jit(solution)/shard_map/all_gather | solution.py:53
  148.0 8.1 %all-gather.5 = f32[2,4,24]{2,1,0:T(4,128)S(1)} all-gather(f32[1,4,24]{2,1,0:T(4,128)S(1)} %maximum_bitcast_fusion.1), channel_id=3, replica_groups=mesh['hst_0'=8,'hst_1'=2,'local_0'=4,'local_1'=4] {'hst_1'}, dimensions={0}, use_global_device_ids=true | all-gather | bytes 1152 | tf_op jit(solution)/shard_map/all_gather | solution.py:53
  156.1 8.3 %all-gather.6 = f32[4,4,24]{2,1,0:T(4,128)S(1)} all-gather(f32[1,4,24]{2,1,0:T(4,128)S(1)} %maximum_bitcast_fusion.2), channel_id=4, replica_groups=mesh['hst_0'=8,'hst_1'=2,'local_0'=4,'local_1'=4] {'local_0'}, dimensions={0}, use_global_device_ids=true | all-gather | bytes 1920 | tf_op jit(solution)/shard_map/all_gather | solution.py:53
  164.5 8.1 %all-gather.7 = f32[4,4,24]{2,1,0:T(4,128)S(1)} all-gather(f32[1,4,24]{2,1,0:T(4,128)S(1)} %maximum_bitcast_fusion.3), channel_id=5, replica_groups=mesh['hst_0'=8,'hst_1'=2,'local_0'=4,'local_1'=4] {'local_1'}, dimensions={0}, use_global_device_ids=true | all-gather | bytes 1920 | tf_op jit(solution)/shard_map/all_gather | solution.py:53
  172.6 1.1 fusion.121
  173.7 0.3 reshape.1574
  174.0 0.3 copy.48
  174.4 0.5 reshape.1592
  174.9 8.9 %all_to_all.32 = f32[4,1,24576]{2,1,0:T(1,128)S(1)} all-to-all(f32[4,1,24576]{2,1,0:T(1,128)S(1)} %reshape.1592), channel_id=1, replica_groups=mesh['hst_0'=8,'hst_1'=2,'local_0'=4,'local_1'=4] {'local_1'}, dimensions={0} | all-to-all | bytes 786432 | tf_op jit(solution)/shard_map/all_to_all | solution.py:35
  183.7 0.5 broadcast.6
  184.2 1.7 reduce.2
  185.9 0.4 reshape.1593
  186.4 0.3 copy.51
  186.7 1.0 reshape.1594
  187.7 14.0 %all-to-all-start.5 = ((f32[64,1,384]{2,1,0:T(1,128)}), f32[64,1,384]{2,1,0:T(1,128)S(1)}, u32[]{:S(2)}, u32[]{:S(2)}) async-start(f32[64,1,384]{2,1,0:T(1,128)} %reshape.1594), calls=%async_computation.5 | async-start | bytes 196608 | tf_op jit(solution)/shard_map/all_to_all | solution.py:42
  201.7 1.2 fusion.1
  202.9 1.4 copy.52
  204.2 7.0 %all-to-all-done.5 = f32[64,1,384]{2,1,0:T(1,128)S(1)} async-done(((f32[64,1,384]{2,1,0:T(1,128)}), f32[64,1,384]{2,1,0:T(1,128)S(1)}, u32[]{:S(2)}, u32[]{:S(2)}) %all-to-all-start.5) | async-done | bytes 98336 | tf_op jit(solution)/shard_map/all_to_all | solution.py:42
  211.2 0.8 reduce.3
  212.0 0.3 reshape.1595
  212.4 0.7 bitcast_reduce_fusion.1
  (19 shorter events, 0.4 us)
Async XLA Ops:
  0.6 107.2 %copy-start = (bf16[4096,125]{1,0:T(8,128)(2,1)S(1)}, bf16[4096,125]{1,0:T(8,128)(2,1)}, u32[]{:S(2)}) copy-start(bf16[4096,125]{1,0:T(8,128)(2,1)} %param.9) | copy-start | bytes 3072004
  3.2 34.2 %all-to-all-start.2 = ((f32[4,1,1]{2,1,0:T(1,128)}), f32[4,1,1]{2,1,0:T(1,128)S(1)}, u32[]{:S(2)}, u32[]{:S(2)}) async-start(f32[4,1,1]{2,1,0:T(1,128)} %broadcast_in_dim.4), calls=%async_computation.2 | async-start | bytes 4096 | tf_op jit(solution)/shard_map/all_to_all | solution.py:12
  8.0 4.9 %copy-start.1 = (bf16[2,24,32000]{2,1,0:T(8,128)(2,1)S(1)}, bf16[2,24,32000]{2,1,0:T(8,128)(2,1)}, u32[]{:S(2)}) copy-start(bf16[2,24,32000]{2,1,0:T(8,128)(2,1)} %param.5) | copy-start | bytes 9216004
  37.4 40.6 %all-to-all-start = ((f32[4,64,24,125]{3,1,2,0:T(8,128)}), f32[4,64,24,125]{3,1,2,0:T(8,128)}, u32[]{:S(2)}, u32[]{:S(2)}) async-start(f32[4,64,24,125]{3,1,2,0:T(8,128)} %copy.43), calls=%async_computation | async-start | bytes 6291456 | tf_op jit(solution)/shard_map/all_to_all | solution.py:35
  79.3 23.5 %all-to-all-start.3 = ((f32[64,1,1]{2,1,0:T(1,128)}), f32[64,1,1]{2,1,0:T(1,128)S(1)}, u32[]{:S(2)}, u32[]{:S(2)}) async-start(f32[64,1,1]{2,1,0:T(1,128)} %broadcast_in_dim.5), calls=%async_computation.3 | async-start | bytes 65536 | tf_op jit(solution)/shard_map/all_to_all | solution.py:12
  93.6 14.2 %copy-start.2 = (bf16[24,4096]{1,0:T(8,128)(2,1)S(1)}, bf16[24,4096]{1,0:T(8,128)(2,1)}, u32[]{:S(2)}) copy-start(bf16[24,4096]{1,0:T(8,128)(2,1)} %param.8) | copy-start | bytes 589828
  102.8 27.8 %all-to-all-start.1 = ((f32[64,24,125]{2,1,0:T(8,128)}), f32[64,24,125]{2,1,0:T(8,128)S(1)}, u32[]{:S(2)}, u32[]{:S(2)}) async-start(f32[64,24,125]{2,1,0:T(8,128)} %copy.45), calls=%async_computation.1 | async-start | bytes 1572864 | tf_op jit(solution)/shard_map/all_to_all | solution.py:42
  187.7 23.5 %all-to-all-start.5 = ((f32[64,1,384]{2,1,0:T(1,128)}), f32[64,1,384]{2,1,0:T(1,128)S(1)}, u32[]{:S(2)}, u32[]{:S(2)}) async-start(f32[64,1,384]{2,1,0:T(1,128)} %reshape.1594), calls=%async_computation.5 | async-start | bytes 196608 | tf_op jit(solution)/shard_map/all_to_all | solution.py:42
where the time goes:
time: 214 us; the launch traced here: 213 us
  waiting for transfers between devices  69.4 us (32%)
  blocking collectives  49 us (23%)
  starting transfers between devices  42.7 us (20%)
  local copies, waits for them, and re-layouts  31.9 us (15%)
  other arithmetic  11.1 us (5%)
  matrix products  8.22 us (4%)
    all_gather x4, blocking collectives, gathered_once(): both, at, found = (lax.all_gather(jnp.concatenate(lines), axis), 0, {})  40.1 us
    all_to_all x1, waiting for transfers between devices, sum_at_owner(): lax.all_to_all(blocks, axis, split_axis=0, concat_axis=0, tiled=True)  35.4 us
    all_to_all x2, waiting for transfers between devices, sum_in_two_steps(): return jnp.sum(lax.all_to_all(own, far, 0, 0, tiled=True), axis=0)  28.5 us
    all_to_all x2, starting transfers between devices, sent_to_all(): lax.all_to_all(jnp.broadcast_to(shard[None], (devices, *shard.shape)), ax...  19.1 us
    all_to_all x2, starting transfers between devices, sum_in_two_steps(): return jnp.sum(lax.all_to_all(own, far, 0, 0, tiled=True), axis=0)  19 us
    reshape x5, local copies, waits for them, and re-layouts, cut_along(): shard.reshape(*lengths[:dim], devices, lengths[dim] // devices, *lengths[...  16.7 us
    all_to_all x1, blocking collectives, sum_at_owner(): lax.all_to_all(blocks, axis, split_axis=0, concat_axis=0, tiled=True)  8.87 us
    dot_general x2, matrix products, per_device(): jnp.dot(selector, teacher_logits[client], preferred_element_type=jnp.floa...  5.58 us
  transfers between devices with their start and end apart: 5, of which 4 were waited for; matrix products, arithmetic and copies ran while one was open for 18% of the time, Pallas kernels for 0%

commit v1 on v0

v1 whole, which is shorter than its diff:
```python
import jax
import jax.numpy as jnp
from jax import lax
from jax.experimental import pallas as pl
from jax.experimental.pallas import tpu as pltpu
from jax.sharding import PartitionSpec as P

MESH = pl.DeviceIdType.MESH
F32 = jnp.float32
BF16 = jnp.bfloat16
SAMPLES = 24
VOCAB = 32000
WIDTH = 4096
SLICE = 125
LANES = 128
SCALE = 32768.0 / SAMPLES
OFFSETS = (2, 1, 3, 0)
PARTS = 5
PART_COLUMNS = VOCAB // PARTS
STEP_COLUMNS = 1280
STEPS = PART_COLUMNS // STEP_COLUMNS
LOW = -3.0e38


def remote(src, dst, send_sem, recv_sem, hst, loc):
    return pltpu.make_async_remote_copy(
        src_ref=src,
        dst_ref=dst,
        send_sem=send_sem,
        recv_sem=recv_sem,
        device_id={"hst": hst, "local": loc},
        device_id_type=MESH,
    )


def lane_index(rows):
    return lax.broadcasted_iota(jnp.int32, (rows, LANES), 1)


def masked_stats(values):
    valid = lane_index(SAMPLES) < SLICE
    top = jnp.max(jnp.where(valid, values, LOW), axis=1, keepdims=True)
    weights = jnp.where(valid, jnp.exp(values - top), 0.0)
    return top, jnp.sum(weights, axis=1, keepdims=True), weights


def packed_stats(top, total):
    lane = lane_index(8)
    tile = jnp.zeros((8, LANES), F32)
    for r in range(3):
        tile = jnp.where((lane >= 16 * r) & (lane < 16 * r + 16), top[8 * r : 8 * r + 8], tile)
        low = 48 + 16 * r
        tile = jnp.where((lane >= low) & (lane < low + 16), total[8 * r : 8 * r + 8], tile)
    return tile


def split_two(weights):
    high = weights.astype(BF16)
    low = (weights - high.astype(F32)).astype(BF16)
    return jnp.concatenate([high, low], axis=0)[:, :SLICE]


def partial_blocks(both, w_perm, core, out, stats):
    rows = w_perm[core].reshape(WIDTH // 2, SLICE)
    product = lax.dot_general(both, rows, (((1,), (1,)), ((), ())), preferred_element_type=F32)
    product = product[:SAMPLES] + product[SAMPLES:]
    for b in range(16):
        out[b, 0:SAMPLES, :] = product[:, LANES * b : LANES * (b + 1)]
        out[b, SAMPLES:32, :] = stats


def factors(stat, joined):
    scale = jnp.exp(stat - joined)
    return scale, [scale[:, 16 * r : 16 * r + 1] for r in range(3)]


def join_cores(own, came):
    mine, theirs = own[0, SAMPLES:32, :], came[0, SAMPLES:32, :]
    joined = jnp.maximum(mine, theirs)
    f_mine, mine_rows = factors(mine, joined)
    f_theirs, their_rows = factors(theirs, joined)
    total = mine * pltpu.roll(f_mine, 48, 1) + theirs * pltpu.roll(f_theirs, 48, 1)
    stats = jnp.where(lane_index(8) < 48, joined, total)
    for b in range(16):
        for r in range(3):
            rows = slice(8 * r, 8 * r + 8)
            own[b, rows, :] = own[b, rows, :] * mine_rows[r] + came[b, rows, :] * their_rows[r]
        own[b, SAMPLES:32, :] = stats


def join_plane(own, here, came):
    mine = own[here]
    stats = [mine[SAMPLES:32]] + [came[k, SAMPLES:32, :] for k in range(1, 16)]
    joined = stats[0]
    for stat in stats[1:]:
        joined = jnp.maximum(joined, stat)
    total = jnp.zeros((8, LANES), F32)
    sums = [jnp.zeros((8, LANES), F32) for _ in range(3)]
    for k in range(16):
        scale, rows = factors(stats[k], joined)
        total = total + stats[k] * pltpu.roll(scale, 48, 1)
        for r in range(3):
            block = mine[8 * r : 8 * r + 8] if k == 0 else came[k, 8 * r : 8 * r + 8, :]
            sums[r] = sums[r] + block * rows[r]
    tops = [joined[:, 16 * r : 16 * r + 1] for r in range(3)]
    totals = [total[:, 48 + 16 * r : 49 + 16 * r] for r in range(3)]
    return sums, tops, totals


def kernel(
    counts, ids, logits_hbm, hidden_hbm, weight_hbm, perm_hbm,
    grad_ref, hidden_out,
    x_in, local, hidden, weight, w_perm,
    to_core, own, from_core,
    fwd1, got1, second, fwd2, got2, third, from_z,
    t_own, t_to, t_from, t_plane, s_own, s_to, s_from, s_plane,
    z_to, z_from, teacher, student,
    load_sems, core_send, core_recv, ring_send, ring_recv,
    z_send, z_recv, side_send, side_recv, plane_send, plane_recv, last_send, last_recv,
):
    hst, loc = lax.axis_index("hst"), lax.axis_index("local")
    z, c = hst // 2, hst % 2
    y, x = loc // 4, loc % 4
    other = z * 2 + (1 - c)

    barrier = pltpu.get_barrier_semaphore()

    def greet(to_hst, to_loc):
        pl.semaphore_signal(
            barrier, inc=1, device_id={"hst": to_hst, "local": to_loc}, device_id_type=MESH
        )

    greet(other, loc)
    for k in range(1, 16):
        greet(hst, ((y + k // 4) % 4) * 4 + (x + k % 4) % 4)
    for k in range(1, 8):
        greet(((z + k) % 8) * 2 + c, loc)

    loads = [
        pltpu.make_async_copy(
            logits_hbm.at[:, pl.ds(k * PART_COLUMNS, PART_COLUMNS)],
            x_in.at[:, pl.ds(k * PART_COLUMNS, PART_COLUMNS)],
            load_sems.at[k],
        )
        for k in range(PARTS)
    ]
    late = [
        pltpu.make_async_copy(hidden_hbm, hidden, load_sems.at[PARTS]),
        pltpu.make_async_copy(weight_hbm, weight, load_sems.at[PARTS + 1]),
    ]
    for a in range(8):
        for b in range(2):
            late.append(
                pltpu.make_async_copy(
                    perm_hbm.at[a, b], w_perm.at[b, :, :, a], load_sems.at[PARTS + 2 + 2 * a + b]
                )
            )
    for load in loads + late:
        load.start()

    place = lax.broadcasted_iota(jnp.int32, (48, SAMPLES), 0)
    first = (ids[0:1, :] == place).astype(F32)
    second_half = (ids[1:2, :] == place - SAMPLES).astype(F32)
    selector = jnp.concatenate([first, second_half], axis=1).astype(BF16)
    count0 = counts[0].astype(F32)
    count1 = counts[1].astype(F32)
    count_sum = count0 + count1

    for k in range(PARTS):
        loads[k].wait()

        def multiply(i, carry, k=k):
            at = pl.multiple_of(k * PART_COLUMNS + i * STEP_COLUMNS, LANES)
            aligned = jnp.dot(
                selector, x_in[:, pl.ds(at, STEP_COLUMNS)], preferred_element_type=F32
            )
            both = count0 * aligned[:SAMPLES] + count1 * aligned[SAMPLES:]
            tile = (k * PART_COLUMNS + i * STEP_COLUMNS) // LANES
            for j in range(STEP_COLUMNS // LANES):
                local[tile + j] = both[:, LANES * j : LANES * (j + 1)]
            return carry

        lax.fori_loop(0, STEPS, multiply, 0)

    pl.semaphore_wait(barrier, 23)

    lane = lane_index(SAMPLES)

    def sliced(device):
        start = device * SLICE
        tile, shift = start // LANES, start % LANES
        back = (LANES - shift) % LANES
        low = pltpu.roll(local[tile], back, 1)
        high = pltpu.roll(local[tile + 1], back, 1)
        block = jnp.where(lane < LANES - shift, low, high)
        return jnp.where(lane < SLICE, block, count_sum)

    core_copies = []
    for k in range(4):
        def cut(i, carry, k=k):
            color, half, kk, zlo = i // 16, (i // 8) % 2, (i // 2) % 4, i % 2
            along = (x * (1 - color) + y * color + OFFSETS[k]) % 4
            across = (y * (1 - color) + x * color + kk) % 4
            to_x = along * (1 - color) + across * color
            to_y = across * (1 - color) + along * color
            to_z = color * 4 + half * 2 + zlo
            base = to_z * 32 + to_y * 4 + to_x
            to_core[32 * k + i] = sliced(base + 16 * (1 - c))
            own[32 * k + i] = sliced(base + 16 * c)
            return carry

        lax.fori_loop(0, 32, cut, 0, unroll=2)
        part = pl.ds(32 * k, 32)
        copy = remote(
            to_core.at[part], from_core.at[part], core_send.at[k], core_recv.at[k], other, loc
        )
        copy.start()
        core_copies.append(copy)

    x_next, x_back = y * 4 + (x + 1) % 4, y * 4 + (x + 3) % 4
    y_next, y_back = ((y + 1) % 4) * 4 + x, ((y + 3) % 4) * 4 + x

    def add_range(dst, at, src, src_at, count):
        def add(i, carry):
            dst[at + i] = dst[at + i] + src[src_at + i]
            return carry

        lax.fori_loop(0, count, add, 0, unroll=2)

    sent = list(core_copies)

    def start(copy):
        copy.start()
        sent.append(copy)
        return copy

    ways1 = ((x_next, x_back), (y_next, y_back))
    forwards1, direct1, relayed1 = {}, {}, {}

    def sem(stage, color, kind):
        return stage * 12 + color * 6 + kind

    def ring(stage, color, kind, src, dst, to):
        n = sem(stage, color, kind)
        return start(remote(src, dst, ring_send.at[n], ring_recv.at[n], hst, to))

    core_copies[0].wait_recv()
    add_range(own, 0, from_core, 0, 32)
    for color in range(2):
        ahead, behind = ways1[color]
        base = 16 * color
        for half, to in ((0, ahead), (1, behind)):
            forwards1[color, half] = ring(
                0, color, half, own.at[pl.ds(base + 8 * half, 8)], fwd1.at[2 * color + half], to
            )
    for k, half in ((1, 1), (2, 0)):
        core_copies[k].wait_recv()
        add_range(own, 32 * k, from_core, 32 * k, 32)
        for color in range(2):
            to = ways1[color][k - 1]
            direct1[color, k] = ring(
                0, color, 1 + k, own.at[pl.ds(32 * k + 16 * color + 8 * half, 8)],
                got1.at[2 * color + k - 1, pl.ds(8 * half, 8)], to,
            )
    core_copies[3].wait_recv()
    add_range(own, 96, from_core, 96, 32)
    for k, half in ((1, 0), (2, 1)):
        for color in range(2):
            forwards1[color, half].wait_recv()
            at = 32 * k + 16 * color + 8 * half
            for i in range(8):
                own[at + i] = own[at + i] + fwd1[2 * color + half, i]
            relayed1[color, k] = ring(
                0, color, 3 + k, own.at[pl.ds(at, 8)],
                got1.at[2 * color + k - 1, pl.ds(8 * half, 8)], ways1[color][k - 1],
            )

    for load in late:
        load.wait()
    values = jnp.dot(hidden[...], weight[...], preferred_element_type=F32)
    values = jnp.concatenate([values, jnp.zeros((SAMPLES, 3), F32)], axis=1)
    student[...] = values
    top, total, weights = masked_stats(values)
    both = split_two(weights)
    stats = packed_stats(top, total)
    partial_blocks(both, w_perm, 1 - c, s_to, stats)
    side_s = start(remote(s_to, s_from, side_send.at[0], side_recv.at[0], other, loc))
    partial_blocks(both, w_perm, c, s_own, stats)
    side_s.wait_recv()
    join_cores(s_own, s_from)

    for color in range(2):
        for k in (1, 2):
            direct1[color, k].wait_recv()
            relayed1[color, k].wait_recv()
        for i in range(16):
            second[color, i] = (
                own[96 + 16 * color + i] + got1[2 * color, i] + got1[2 * color + 1, i]
            )
    ways2 = ((y_next, y_back), (x_next, x_back))
    forwards2, direct2, relayed2 = {}, {}, {}
    for color in range(2):
        for half in range(2):
            forwards2[color, half] = ring(
                1, color, half, second.at[color, pl.ds(8 * half + 4, 2)],
                fwd2.at[2 * color + half], ways2[color][half],
            )
        for k, half, kk in ((1, 1, 1), (2, 0, 3)):
            direct2[color, k] = ring(
                1, color, 1 + k, second.at[color, pl.ds(8 * half + 2 * kk, 2)],
                got2.at[2 * color + k - 1, pl.ds(2 * half, 2)], ways2[color][k - 1],
            )
    for color in range(2):
        for k, half, kk in ((1, 0, 1), (2, 1, 3)):
            forwards2[color, half].wait_recv()
            at = 8 * half + 2 * kk
            for i in range(2):
                second[color, at + i] = second[color, at + i] + fwd2[2 * color + half, i]
            relayed2[color, k] = ring(
                1, color, 3 + k, second.at[color, pl.ds(at, 2)],
                got2.at[2 * color + k - 1, pl.ds(2 * half, 2)], ways2[color][k - 1],
            )
    for color in range(2):
        for k in (1, 2):
            direct2[color, k].wait_recv()
            relayed2[color, k].wait_recv()
        for half in range(2):
            for i in range(2):
                third[4 * color + 2 * half + i] = (
                    second[color, 8 * half + i]
                    + got2[2 * color, 2 * half + i]
                    + got2[2 * color + 1, 2 * half + i]
                )

    z_copies = []
    for k in (4, 3, 5, 2, 6, 1, 7):
        to_z = (z + k) % 8
        z_copies.append(
            start(remote(third.at[to_z], from_z.at[k], z_send.at[k], z_recv.at[k], to_z * 2 + c, loc))
        )

    def plane(src, dst, which):
        copies = []
        for k in range(1, 16):
            to = ((y + k // 4) % 4) * 4 + (x + k % 4) % 4
            copies.append(
                start(
                    remote(
                        src.at[to], dst.at[k], plane_send.at[16 * which + k],
                        plane_recv.at[16 * which + k], hst, to,
                    )
                )
            )
        return copies

    student_plane = plane(s_own, s_plane, 0)
    for copy in z_copies:
        copy.wait_recv()
    summed = third[z]
    for k in range(1, 8):
        summed = summed + from_z[k]

    ensemble = summed / summed[:, SLICE : SLICE + 1]
    teacher[...] = ensemble
    top, total, weights = masked_stats(ensemble)
    both = split_two(weights)
    stats = packed_stats(top, total)
    partial_blocks(both, w_perm, 1 - c, t_to, stats)
    side_t = start(remote(t_to, t_from, side_send.at[1], side_recv.at[1], other, loc))
    partial_blocks(both, w_perm, c, t_own, stats)
    side_t.wait_recv()
    join_cores(t_own, t_from)
    teacher_plane = plane(t_own, t_plane, 1)

    for copy in student_plane:
        copy.wait_recv()
    s_sums, s_tops, s_totals = join_plane(s_own, loc, s_plane)
    lane8 = lane_index(8)

    def spread(sums, tops, totals, base, tile, tops_tile):
        for r in range(3):
            low = base + 20 * r
            inside = (lane8 >= low) & (lane8 < low + 16)
            ending = (lane8 >= low + 16) & (lane8 < low + 20)
            for k in range(8):
                moved = pltpu.roll(sums[r], (low - 16 * k) % LANES, 1)
                tile[k] = jnp.where(ending, totals[r], jnp.where(inside, moved, tile[k]))
            tops_tile = jnp.where(inside | ending, tops[r], tops_tile)
        return tops_tile

    tiles = [jnp.zeros((8, LANES), F32) for _ in range(8)]
    tops_tile = spread(s_sums, s_tops, s_totals, 60, tiles, jnp.zeros((8, LANES), F32))
    for copy in teacher_plane:
        copy.wait_recv()
    t_sums, t_tops, t_totals = join_plane(t_own, loc, t_plane)
    tops_tile = spread(t_sums, t_tops, t_totals, 0, tiles, tops_tile)
    for k in range(8):
        z_to[k, 0:8, :] = tiles[k]
        z_to[k, 8:16, :] = tops_tile
    last_copies = []
    for k in (4, 3, 5, 2, 6, 1, 7):
        to_z = (z + k) % 8
        last_copies.append(
            start(remote(z_to.at[to_z], z_from.at[k], last_send.at[k], last_recv.at[k], to_z * 2 + c, loc))
        )
    for copy in last_copies:
        copy.wait_recv()
    mine = z_to[z]
    pieces = [mine] + [z_from[k] for k in range(1, 8)]
    joined = pieces[0][8:16]
    for piece in pieces[1:]:
        joined = jnp.maximum(joined, piece[8:16])
    sums = jnp.zeros((8, LANES), F32)
    for piece in pieces:
        sums = sums + piece[0:8] * jnp.exp(piece[8:16] - joined)

    for r in range(3):
        t_low, s_low = 20 * r, 60 + 20 * r
        t_top, s_top = joined[:, t_low : t_low + 1], joined[:, s_low : s_low + 1]
        t_total = sums[:, t_low + 16 : t_low + 17]
        s_total = sums[:, s_low + 16 : s_low + 17]
        rows = slice(8 * r, 8 * r + 8)
        t_part = pltpu.roll(sums, (LANES - t_low) % LANES, 1) / t_total
        s_part = pltpu.roll(sums, (LANES - s_low) % LANES, 1) / s_total
        hidden_out[rows, :] = (SCALE * (s_part - t_part))[:, :16]
        s_prob = jnp.exp(student[rows, :] - s_top) / s_total
        t_prob = jnp.exp(teacher[rows, :] - t_top) / t_total
        grad_ref[rows, :] = (SCALE * (s_prob - t_prob))[:, :SLICE]

    for copy in sent:
        copy.wait_send()


def per_device(teacher_logits, sample_ids, client_counts, student_hidden, student_weight):
    logits = teacher_logits.reshape(2 * SAMPLES, VOCAB)
    perm = student_weight.reshape(8, 2, 4, 4, 16, SLICE)
    any_spec = pl.BlockSpec(memory_space=pltpu.HBM)
    vmem = pl.BlockSpec(memory_space=pltpu.VMEM)
    block = (SAMPLES, LANES)
    tall = (16, 32, LANES)
    dma = pltpu.SemaphoreType.DMA
    grad, grad_hidden = pl.pallas_call(
        kernel,
        out_shape=(
            jax.ShapeDtypeStruct((SAMPLES, SLICE), F32),
            jax.ShapeDtypeStruct((SAMPLES, 16), F32),
        ),
        in_specs=[pl.BlockSpec(memory_space=pltpu.SMEM), vmem] + [any_spec] * 4,
        out_specs=(vmem, vmem),
        scratch_shapes=[
            pltpu.VMEM((2 * SAMPLES, VOCAB), BF16),
            pltpu.VMEM((VOCAB // LANES + 2, *block), F32),
            pltpu.VMEM((SAMPLES, WIDTH), BF16),
            pltpu.VMEM((WIDTH, SLICE), BF16),
            pltpu.VMEM((2, 4, 4, 8, 16, SLICE), BF16),
            pltpu.VMEM((128, *block), F32),
            pltpu.VMEM((128, *block), F32),
            pltpu.VMEM((128, *block), F32),
            pltpu.VMEM((4, 8, *block), F32),
            pltpu.VMEM((4, 16, *block), F32),
            pltpu.VMEM((2, 16, *block), F32),
            pltpu.VMEM((4, 2, *block), F32),
            pltpu.VMEM((4, 4, *block), F32),
            pltpu.VMEM((8, *block), F32),
            pltpu.VMEM((8, *block), F32),
            pltpu.VMEM(tall, F32),
            pltpu.VMEM(tall, F32),
            pltpu.VMEM(tall, F32),
            pltpu.VMEM(tall, F32),
            pltpu.VMEM(tall, F32),
            pltpu.VMEM(tall, F32),
            pltpu.VMEM(tall, F32),
            pltpu.VMEM(tall, F32),
            pltpu.VMEM((8, 16, LANES), F32),
            pltpu.VMEM((8, 16, LANES), F32),
            pltpu.VMEM(block, F32),
            pltpu.VMEM(block, F32),
            dma((PARTS + 18,)),
            dma((4,)),
            dma((4,)),
            dma((24,)),
            dma((24,)),
            dma((8,)),
            dma((8,)),
            dma((2,)),
            dma((2,)),
            dma((32,)),
            dma((32,)),
            dma((8,)),
            dma((8,)),
        ],
        compiler_params=pltpu.CompilerParams(
            collective_id=0, has_side_effects=True, vmem_limit_bytes=48 * 1024 * 1024
        ),
        name="distill",
    )(client_counts, sample_ids, logits, student_hidden, student_weight, perm)
    grad_weight = lax.dot_general(
        student_hidden, grad.astype(BF16), (((0,), (0,)), ((), ())), preferred_element_type=F32
    ).astype(BF16)
    return grad_weight, grad_hidden


def solution(mesh):
    both = ("hst", "local")
    return jax.shard_map(
        per_device,
        mesh=mesh,
        in_specs=(P(both, None, None), P(both, None), P(both), P(), P(None, both)),
        out_specs=(P(None, both), P(None, both)),
        check_vma=False,
    )
```

time: 214 us -> 66.6 us (0.31)
  waiting for transfers between devices: 69.4 us -> 0 us
  Pallas kernels: 0 us -> 57.8 us
  blocking collectives: 49 us -> 0 us
  starting transfers between devices: 42.7 us -> 0 us
  local copies, waits for them, and re-layouts: 31.9 us -> 7.38 us
  other arithmetic: 11.1 us -> 0 us
  matrix products: 8.22 us -> 0.47 us
    all_to_all x5 -> x0, waiting for transfers between devices: 69.4 us -> none  [the longest x1 35.4 us: sum_at_owner(): lax.all_to_all(blocks, axis, split_axis=0, concat_axis=0, tiled=True)]
    pallas_call x0 -> x1, Pallas kernels: none -> 57.8 us  [per_device(): pl.pallas_call(kernel, out_shape=(jax.ShapeDtypeStruct((SAMPLES, SLICE),...]
    all_to_all x5 -> x0, starting transfers between devices: 42.7 us -> none  [the longest x2 19.1 us: sent_to_all(): lax.all_to_all(jnp.broadcast_to(shard[None], (devices, *shard.shape)), ax...]
    all_gather x4 -> x0, blocking collectives: 40.1 us -> none  [gathered_once(): both, at, found = (lax.all_gather(jnp.concatenate(lines), axis), 0, {})]
    reshape x5 -> x0, local copies, waits for them, and re-layouts: 16.7 us -> none  [cut_along(): shard.reshape(*lengths[:dim], devices, lengths[dim] // devices, *lengths[...]
    all_to_all x1 -> x0, blocking collectives: 8.87 us -> none  [sum_at_owner(): lax.all_to_all(blocks, axis, split_axis=0, concat_axis=0, tiled=True)]
    dot_general x5 -> x1, matrix products: 8.22 us -> 0.47 us  [per_device(): lax.dot_general(student_hidden, grad.astype(BF16), (((0,), (0,)), ((), ()...]
    reduce_sum x9 -> x0, other arithmetic: 6.87 us -> none  [the longest x2 2.44 us: sum_at_owner(): return arrived.sum(axis=0)]
  transfers between devices with their start and end apart: 5 -> 0, of which waited for: 4 -> 0; matrix products, arithmetic and copies ran while one was open for 18% -> 0% of each run, Pallas kernels for 0% -> 0%
where the time goes in v1:
time: 66.6 us; the launch traced here: 66.3 us
  Pallas kernels  57.8 us (87%)
  local copies, waits for them, and re-layouts  7.38 us (11%)
    pallas_call x1, Pallas kernels, per_device(): pl.pallas_call(kernel, out_shape=(jax.ShapeDtypeStruct((SAMPLES, SLICE),...  57.8 us
    unnamed x14, local copies, waits for them, and re-layouts  7.38 us

profile of v1, /device:TPU:1, one launch (start us, length us, event | category | flops | bytes accessed | tf_op | source)
XLA Modules:
  0.0 66.3 jit_solution(4992147285445593168)
XLA Ops:
  0.6 0.0 copy-start
  0.6 1.2 %copy-done = bf16[4096,125]{1,0:T(8,128)(2,1)S(1)} copy-done((bf16[4096,125]{1,0:T(8,128)(2,1)S(1)}, bf16[4096,125]{1,0:T(8,128)(2,1)}, u32[]{:S(2)}) %copy-start) | copy-done | bytes 1024024
  1.9 0.0 copy-start.1
  1.9 1.9 %copy-done.1 = bf16[2,24,32000]{2,1,0:T(8,128)(2,1)S(1)} copy-done((bf16[2,24,32000]{2,1,0:T(8,128)(2,1)S(1)}, bf16[2,24,32000]{2,1,0:T(8,128)(2,1)}, u32[]{:S(2)}) %copy-start.1) | copy-done | bytes 3072024
  3.7 0.0 copy-start.2
  3.7 0.9 %copy-done.2 = bf16[24,4096]{1,0:T(8,128)(2,1)S(1)} copy-done((bf16[24,4096]{1,0:T(8,128)(2,1)S(1)}, bf16[24,4096]{1,0:T(8,128)(2,1)}, u32[]{:S(2)}) %copy-start.2) | copy-done | bytes 196632
  4.7 0.0 copy-start.4
  4.7 0.7 %copy-done.4 = s32[2,24]{1,0:T(2,128)S(1)} copy-done((s32[2,24]{1,0:T(2,128)S(1)}, s32[2,24]{1,0:T(2,128)}, u32[]{:S(2)}) %copy-start.4) | copy-done | bytes 216
  5.3 0.0 copy-start.5
  5.3 0.7 copy-done.5
  6.0 0.0 copy-start.3
  6.0 57.8 %distill.1 = (f32[24,125]{1,0:T(8,128)S(1)}, f32[24,16]{1,0:T(8,128)S(1)}) custom-call(s32[2]{0:T(128)S(1)} %copy-done.5, s32[2,24]{1,0:T(2,128)S(1)} %copy-done.4, bf16[48,32000]{1,0:T(8,128)(2,1)S(1)} %bitcast.6, bf16[24,4096]{1,0:T(8,128)(2,1)S(1)} %copy-done.2, bf16[4096,125]{1,0:T(8,128)(2,1)S(1)} %copy-done, bf16[8,2,4,4,16,125]{5,4,3,2,1,0:T(8,128)(2,1)S(1)} %bitcast.5), custom_call_target="tpu_custom_call" | custom-call | tf_op jit(solution)/shard_map/distill/pallas_call | solution.py:442
  63.8 0.7 %copy.8 = f32[24,16]{0,1:T(8,128)} copy(f32[24,16]{1,0:T(8,128)S(1)} %get-tuple-element.7) | data formatting | bytes 3072
  64.5 0.0 copy-done.3
  64.5 0.5 fusion
  65.0 1.4 %copy.7 = bf16[4096,125]{1,0:T(8,128)(2,1)} copy(bf16[4096,125]{0,1:T(8,128)(2,1)S(1)} %fusion) | data formatting | bytes 2048000
Async XLA Ops:
  0.6 1.2 %copy-start = (bf16[4096,125]{1,0:T(8,128)(2,1)S(1)}, bf16[4096,125]{1,0:T(8,128)(2,1)}, u32[]{:S(2)}) copy-start(bf16[4096,125]{1,0:T(8,128)(2,1)} %weight_hbm.1) | copy-start | bytes 3072004
  1.9 1.9 %copy-start.1 = (bf16[2,24,32000]{2,1,0:T(8,128)(2,1)S(1)}, bf16[2,24,32000]{2,1,0:T(8,128)(2,1)}, u32[]{:S(2)}) copy-start(bf16[2,24,32000]{2,1,0:T(8,128)(2,1)} %param.5) | copy-start | bytes 9216004
  3.7 0.9 %copy-start.2 = (bf16[24,4096]{1,0:T(8,128)(2,1)S(1)}, bf16[24,4096]{1,0:T(8,128)(2,1)}, u32[]{:S(2)}) copy-start(bf16[24,4096]{1,0:T(8,128)(2,1)} %hidden_hbm.1) | copy-start | bytes 589828
  4.7 0.7 %copy-start.4 = (s32[2,24]{1,0:T(2,128)S(1)}, s32[2,24]{1,0:T(2,128)}, u32[]{:S(2)}) copy-start(s32[2,24]{1,0:T(2,128)} %ids.1) | copy-start | bytes 580
  5.3 0.7 copy-start.5
  6.0 58.5 %copy-start.3 = (bf16[24,4096]{1,0:T(8,128)(2,1)S(1)}, bf16[24,4096]{1,0:T(8,128)(2,1)}, u32[]{:S(2)}) copy-start(bf16[24,4096]{1,0:T(8,128)(2,1)} %hidden_hbm.1) | copy-start | bytes 589828

commit v2 on v0

v2 whole, which is shorter than its diff:
```python
import jax
import jax.numpy as jnp
from jax import lax
from jax.experimental import pallas as pl
from jax.experimental.pallas import tpu as pltpu
from jax.sharding import PartitionSpec as P

MESH = pl.DeviceIdType.MESH
F32 = jnp.float32
BF16 = jnp.bfloat16
SAMPLES = 24
VOCAB = 32000
WIDTH = 4096
SLICE = 125
LANES = 128
SCALE = 32768.0 / SAMPLES
Z_FAR_FIRST = (4, 3, 5, 2, 6, 1, 7)
FAR_FIRST = (10, 6, 9, 11, 14, 2, 8, 5, 7, 13, 15, 1, 3, 4, 12)
STEP_COLUMNS = 512
STEPS = tuple(-(-min(4000 * (k + 1) + LANES, VOCAB) // STEP_COLUMNS) for k in range(8))
PARTS = 8
WINDOW = 17
LAG = 5
LOW = -3.0e38


def remote(src, dst, send_sem, recv_sem, hst, loc):
    return pltpu.make_async_remote_copy(
        src_ref=src,
        dst_ref=dst,
        send_sem=send_sem,
        recv_sem=recv_sem,
        device_id={"hst": hst, "local": loc},
        device_id_type=MESH,
    )


def lane_index(rows):
    return lax.broadcasted_iota(jnp.int32, (rows, LANES), 1)


def masked_top(values):
    return jnp.max(
        jnp.where(lane_index(SAMPLES) < SLICE, values, LOW), axis=1, keepdims=True
    )


def weighted_product(values, top, rows):
    valid = lane_index(SAMPLES) < SLICE
    weights = jnp.where(valid, jnp.exp(values - top), 0.0)
    product = lax.dot_general(
        split_two(weights), rows, (((1,), (1,)), ((), ())), preferred_element_type=F32
    )
    return jnp.sum(weights, axis=1, keepdims=True), product[:SAMPLES] + product[SAMPLES:]


def packed_stats(top, total):
    lane = lane_index(8)
    tile = jnp.zeros((8, LANES), F32)
    for r in range(3):
        tile = jnp.where((lane >= 16 * r) & (lane < 16 * r + 16), top[8 * r : 8 * r + 8], tile)
        low = 48 + 16 * r
        tile = jnp.where((lane >= low) & (lane < low + 16), total[8 * r : 8 * r + 8], tile)
    return tile


def split_two(weights):
    high = weights.astype(BF16)
    low = (weights - high.astype(F32)).astype(BF16)
    return jnp.concatenate([high, low], axis=0)[:, :SLICE]


def own_part(own, rows, out):
    top = masked_top(own)
    total, product = weighted_product(own, top, rows)
    for b in range(16):
        out[b, 0:SAMPLES, :] = product[:, LANES * b : LANES * (b + 1)]
    return top, total


def other_part(top, total, other, rows, out):
    joined = jnp.maximum(top, masked_top(other))
    more, product = weighted_product(other, joined, rows)
    scale = jnp.exp(top - joined)
    stats = packed_stats(joined, total * scale + more)
    for b in range(16):
        out[b, 0:SAMPLES, :] = (
            out[b, 0:SAMPLES, :] * scale + product[:, LANES * b : LANES * (b + 1)]
        )
        out[b, SAMPLES:32, :] = stats


def factors(stat, joined):
    scale = jnp.exp(stat - joined)
    return scale, [scale[:, 16 * r : 16 * r + 1] for r in range(3)]


def join_plane(own, here, came):
    mine = own[here]
    stats = [mine[SAMPLES:32]] + [came[k, SAMPLES:32, :] for k in range(15)]
    joined = stats[0]
    for stat in stats[1:]:
        joined = jnp.maximum(joined, stat)
    total = jnp.zeros((8, LANES), F32)
    sums = [jnp.zeros((8, LANES), F32) for _ in range(3)]
    for k in range(16):
        scale, rows = factors(stats[k], joined)
        total = total + stats[k] * pltpu.roll(scale, 48, 1)
        for r in range(3):
            block = mine[8 * r : 8 * r + 8] if k == 0 else came[k - 1, 8 * r : 8 * r + 8, :]
            sums[r] = sums[r] + block * rows[r]
    tops = [joined[:, 16 * r : 16 * r + 1] for r in range(3)]
    totals = [total[:, 48 + 16 * r : 49 + 16 * r] for r in range(3)]
    return sums, tops, totals


def kernel(
    counts_hbm, ids_hbm, logits_hbm, hidden_hbm, weight_hbm, perm_hbm,
    grad_ref, hidden_out,
    counts, ids, x_in, local, hidden, weight, w_perm,
    count_to, count_from, blocks, from_core,
    got1, second, got2, third, from_z,
    t_own, t_plane, s_own, s_plane, w_to, w_from, w_other,
    z_to, z_from, teacher, student, s_other, t_other,
    load_sems, core_recv, forward_recv, ring_recv, cross_recv, many_recv, send_sems,
):
    hst, loc = lax.axis_index("hst"), lax.axis_index("local")
    z, c = hst // 2, hst % 2
    y, x = loc // 4, loc % 4
    other = z * 2 + (1 - c)

    early = [
        pltpu.make_async_copy(ids_hbm, ids, load_sems.at[PARTS]),
        pltpu.make_async_copy(counts_hbm, counts, load_sems.at[PARTS + 1]),
    ]
    loads = [
        pltpu.make_async_copy(
            logits_hbm.at[:, pl.ds(low, high - low)], x_in.at[:, pl.ds(low, high - low)],
            load_sems.at[k],
        )
        for k, (low, high) in enumerate(
            (STEP_COLUMNS * ((0,) + STEPS)[k], min(STEP_COLUMNS * STEPS[k], VOCAB))
            for k in range(PARTS)
        )
    ]
    for load in early + loads:
        load.start()

    barrier = pltpu.get_barrier_semaphore()

    def greet(to_hst, to_loc):
        pl.semaphore_signal(
            barrier, inc=1, device_id={"hst": to_hst, "local": to_loc}, device_id_type=MESH
        )

    for k in range(1, 8):
        greet(((z + k) % 8) * 2 + c, loc)
    for k in FAR_FIRST:
        greet(hst, ((y + k // 4) % 4) * 4 + (x + k % 4) % 4)
    greet(other, loc)

    late = [
        pltpu.make_async_copy(hidden_hbm, hidden, load_sems.at[PARTS + 2]),
        pltpu.make_async_copy(weight_hbm, weight, load_sems.at[PARTS + 3]),
    ]
    for load in late:
        load.start()
    for a in range(8):
        for b in range(2):
            pltpu.make_async_copy(
                perm_hbm.at[a, b], w_perm.at[b, :, :, a], load_sems.at[PARTS + 4]
            ).start()
    late.append(pltpu.make_async_copy(w_perm, w_perm, load_sems.at[PARTS + 4]))
    for load in early:
        load.wait()

    place = lax.broadcasted_iota(jnp.int32, (SAMPLES, SAMPLES), 0)
    highs, lows = [], []
    for client in range(2):
        chosen = ids[client : client + 1, :] == place
        high = (counts[client] // 256) * 256
        highs.append(jnp.where(chosen, high.astype(F32), 0.0))
        lows.append(jnp.where(chosen, (counts[client] - high).astype(F32), 0.0))
    one = jnp.concatenate(highs + lows, axis=1)
    none = jnp.zeros_like(one)
    selector = jnp.concatenate(
        [jnp.concatenate([one, none], axis=1), jnp.concatenate([none, one], axis=1)], axis=0
    ).astype(BF16)
    count_sum = (counts[0] + counts[1]).astype(F32)
    count_to[...] = jnp.full((8, LANES), count_sum, F32)
    local[VOCAB // LANES] = jnp.zeros((SAMPLES, LANES), F32)
    lane = lane_index(SAMPLES)
    valid = lane < SLICE

    def multiply(step):
        at = step * STEP_COLUMNS
        groups = min(2, (VOCAB - at) // 256)
        columns = [x_in[:, at + 256 * g : at + 256 * (g + 1)] for g in range(groups)]
        stacked = jnp.concatenate([part for part in columns for _ in range(2)], axis=0)
        sums = jnp.dot(
            selector[: 24 * groups, : 96 * groups], stacked, preferred_element_type=F32
        )
        for g in range(groups):
            tile = at // LANES + 2 * g
            local[tile] = sums[24 * g : 24 * g + 24, :LANES]
            local[tile + 1] = sums[24 * g : 24 * g + 24, LANES:]

    places = []
    for color in range(2):
        for k in range(16):
            dx, dy = (k + 4 - x) % 4, (k // 4 + 4 - y) % 4
            along, across = (dy, dx) if color else (dx, dy)
            places.append(along * 4 + across)

    def first_tile(k, side):
        return (32 * k + 16 * side) * SLICE // LANES

    along_x = [y * 4 + (x + n) % 4 for n in range(4)]
    along_y = [((y + n) % 4) * 4 + x for n in range(4)]
    ways = (along_x, along_y)
    core_copies = []

    def send(src, dst, sem, recv_sem, to_hst, to_loc):
        copy = remote(src, dst, send_sems.at[sem], recv_sem, to_hst, to_loc)
        copy.start()
        return copy

    def arrived(ref, recv_sem):
        pltpu.make_async_copy(ref, ref, recv_sem).wait()

    def pair(k, n, half):
        return blocks.at[pl.ds(16 * k + 4 * n + 2 * half, 2)]

    def landing(k, slot, half):
        return got1.at[k, slot, pl.ds(2 * half, 2)]

    def receive_core(k):
        core_copies[k].wait_recv()
        counted = count_from[0:1, :] + count_sum
        for side_c in range(2):

            @pl.when(c == side_c)
            def cut(side_c=side_c):
                base = first_tile(k, side_c)
                for n in range(16):
                    begin = (32 * k + 16 * side_c + n) * SLICE
                    tile, shift = begin // LANES, begin % LANES
                    block = local[tile] + from_core[k, tile - base]
                    if shift + SLICE > LANES:
                        after = local[tile + 1] + from_core[k, tile + 1 - base]
                        block = jnp.where(lane >= shift, block, after)
                    if shift:
                        block = pltpu.roll(block, LANES - shift, 1)
                    blocks[16 * k + places[16 * (k % 2) + n]] = jnp.where(valid, block, counted)

        way = ways[k % 2]
        for half in range(2):
            send(
                pair(k, 2, half), landing(k, 0, half), 1, forward_recv.at[k], hst,
                way[3 if half else 1],
            )

    def direct(k):
        way = ways[k % 2]
        send(pair(k, 1, 1), landing(k, 1, 1), 1, ring_recv.at[k], hst, way[1])
        send(pair(k, 3, 0), landing(k, 2, 0), 1, ring_recv.at[k], hst, way[3])

    def relay(k):
        way = ways[k % 2]
        arrived(got1.at[k, 0], forward_recv.at[k])
        for half, near in ((0, 1), (1, 3)):
            for n in range(2):
                at = 16 * k + 4 * near + 2 * half + n
                blocks[at] = blocks[at] + got1[k, 0, 2 * half + n]
            send(pair(k, near, half), landing(k, 1 + half, half), 1, ring_recv.at[k], hst, way[near])

    for k in range(8):
        loads[k].wait()
        for step in range(((0,) + STEPS)[k], STEPS[k]):
            multiply(step)
        if k == 0:
            pl.semaphore_wait(barrier, 23)
            count_copy = send(count_to, count_from, 9, many_recv.at[6], other, loc)
        window = c * first_tile(k, 0) + (1 - c) * first_tile(k, 1)
        core_copies.append(
            send(
                local.at[pl.ds(window, WINDOW)], from_core.at[k], 0, core_recv.at[k], other, loc
            )
        )
        if k >= LAG:
            if k == LAG:
                count_copy.wait_recv()
            receive_core(k - LAG)
    for k in range(8 - LAG, 8):
        receive_core(k)
    for k in range(8):
        direct(k)
    for k in range(8):
        relay(k)
    for k in range(8):
        arrived(got1.at[k, pl.ds(1, 2)], ring_recv.at[k])
        for n in range(4):
            second[k % 2, n, k // 2] = blocks[16 * k + n] + (got1[k, 1, n] + got1[k, 2, n])
    for n in (2, 1, 3):
        for color in range(2):
            send(
                second.at[color, n], got2.at[color, n - 1], 2, cross_recv.at[color],
                hst, ways[1 - color][n],
            )
    for load in late:
        load.wait()

    @pl.when(c == 0)
    def widen_second():
        w_to[...] = w_perm[1].reshape(WIDTH // 2, SLICE).astype(F32)

    @pl.when(c == 1)
    def widen_first():
        w_to[...] = w_perm[0].reshape(WIDTH // 2, SLICE).astype(F32)

    w_copy = send(w_to, w_from, 5, many_recv.at[0], other, loc)
    student[:, :SLICE] = jnp.dot(hidden[...], weight[...], preferred_element_type=F32)
    student[:, SLICE:] = jnp.zeros((SAMPLES, LANES - SLICE), F32)
    s_copy = send(student, s_other, 7, many_recv.at[1], other, loc)
    for color in range(2):
        arrived(got2.at[color], cross_recv.at[color])
        for item in range(4):
            third[2 * item + color] = (second[color, 0, item] + got2[color, 0, item]) + (
                got2[color, 1, item] + got2[color, 2, item]
            )
    for k in Z_FAR_FIRST:
        to_z = (z + k) % 8
        send(third.at[to_z], from_z.at[k - 1], 3, many_recv.at[2], to_z * 2 + c, loc)
    w_copy.wait_recv()
    w_other[...] = w_from[...].astype(BF16)
    s_copy.wait_recv()
    own_rows = w_perm[c].reshape(WIDTH // 2, SLICE)
    top, total = own_part(student[...], own_rows, s_own)
    other_part(top, total, s_other[...], w_other[...], s_own)

    def plane(src, dst, sem, recv_sem):
        for k in FAR_FIRST:
            to = ((y + k // 4) % 4) * 4 + (x + k % 4) % 4
            send(src.at[to], dst.at[k - 1], sem, recv_sem, hst, to)

    plane(s_own, s_plane, 6, many_recv.at[3])
    arrived(from_z, many_recv.at[2])
    summed = third[z]
    for k in range(7):
        summed = summed + from_z[k]

    ensemble = summed / summed[:, SLICE : SLICE + 1]
    teacher[...] = ensemble
    t_copy = send(teacher, t_other, 10, many_recv.at[7], other, loc)
    top, total = own_part(ensemble, own_rows, t_own)
    t_copy.wait_recv()
    other_part(top, total, t_other[...], w_other[...], t_own)
    plane(t_own, t_plane, 8, many_recv.at[4])

    arrived(s_plane, many_recv.at[3])
    s_sums, s_tops, s_totals = join_plane(s_own, loc, s_plane)
    lane8 = lane_index(8)

    def spread(sums, tops, totals, base, tile, tops_tile):
        for r in range(3):
            low = base + 20 * r
            inside = (lane8 >= low) & (lane8 < low + 16)
            ending = (lane8 >= low + 16) & (lane8 < low + 20)
            for k in range(8):
                moved = pltpu.roll(sums[r], (low - 16 * k) % LANES, 1)
                tile[k] = jnp.where(ending, totals[r], jnp.where(inside, moved, tile[k]))
            tops_tile = jnp.where(inside | ending, tops[r], tops_tile)
        return tops_tile

    tiles = [jnp.zeros((8, LANES), F32) for _ in range(8)]
    tops_tile = spread(s_sums, s_tops, s_totals, 60, tiles, jnp.zeros((8, LANES), F32))
    arrived(t_plane, many_recv.at[4])
    t_sums, t_tops, t_totals = join_plane(t_own, loc, t_plane)
    tops_tile = spread(t_sums, t_tops, t_totals, 0, tiles, tops_tile)
    for k in range(8):
        z_to[k, 0:8, :] = tiles[k]
        z_to[k, 8:16, :] = tops_tile
    for k in Z_FAR_FIRST:
        to_z = (z + k) % 8
        send(z_to.at[to_z], z_from.at[k - 1], 4, many_recv.at[5], to_z * 2 + c, loc)
    arrived(z_from, many_recv.at[5])
    mine = z_to[z]
    pieces = [mine] + [z_from[k] for k in range(7)]
    joined = pieces[0][8:16]
    for piece in pieces[1:]:
        joined = jnp.maximum(joined, piece[8:16])
    sums = jnp.zeros((8, LANES), F32)
    for piece in pieces:
        sums = sums + piece[0:8] * jnp.exp(piece[8:16] - joined)

    for r in range(3):
        t_low, s_low = 20 * r, 60 + 20 * r
        t_top, s_top = joined[:, t_low : t_low + 1], joined[:, s_low : s_low + 1]
        t_total = sums[:, t_low + 16 : t_low + 17]
        s_total = sums[:, s_low + 16 : s_low + 17]
        rows = slice(8 * r, 8 * r + 8)
        t_part = pltpu.roll(sums, (LANES - t_low) % LANES, 1) / t_total
        s_part = pltpu.roll(sums, (LANES - s_low) % LANES, 1) / s_total
        hidden_out[rows, :] = (SCALE * (s_part - t_part))[:, :16]
        s_prob = jnp.exp(student[rows, :] - s_top) / s_total
        t_prob = jnp.exp(teacher[rows, :] - t_top) / t_total
        grad_ref[rows, :] = (SCALE * (s_prob - t_prob))[:, :SLICE]

    for n, ref in enumerate(
        (from_core, got1, got2, from_z, z_from, w_to, s_plane, student, t_plane, count_to, teacher)
    ):
        arrived(ref, send_sems.at[n])


def finish(grad, grad_hidden, hidden, weight_out, hidden_out, rows, sems):
    rounded = grad[...].astype(BF16)
    size = WIDTH // 4
    copies = []
    for k in range(4):
        part = pl.ds(k * size, size)
        rows[part, :] = lax.dot_general(
            hidden[:, part], rounded, (((0,), (0,)), ((), ())), preferred_element_type=F32
        ).astype(BF16)
        copies.append(pltpu.make_async_copy(rows.at[part], weight_out.at[part], sems.at[k]))
        copies[k].start()
    hidden_out[...] = grad_hidden[...].T
    for copy in copies:
        copy.wait()


def per_device(teacher_logits, sample_ids, client_counts, student_hidden, student_weight):
    logits = teacher_logits.reshape(2 * SAMPLES, VOCAB)
    perm = student_weight.reshape(8, 2, 4, 4, 16, SLICE)
    any_spec = pl.BlockSpec(memory_space=pltpu.HBM)
    vmem = pl.BlockSpec(memory_space=pltpu.VMEM)
    block = (SAMPLES, LANES)
    tall = (16, 32, LANES)
    dma = pltpu.SemaphoreType.DMA
    grad, grad_hidden = pl.pallas_call(
        kernel,
        out_shape=(
            pltpu.VMEM((SAMPLES, SLICE), F32),
            pltpu.VMEM((SAMPLES, 16), F32),
        ),
        in_specs=[any_spec] * 6,
        out_specs=(vmem, vmem),
        scratch_shapes=[
            pltpu.SMEM((2,), jnp.int32),
            pltpu.VMEM((2, SAMPLES), jnp.int32),
            pltpu.VMEM((2 * SAMPLES, VOCAB), BF16),
            pltpu.VMEM((VOCAB // LANES + 2, *block), F32),
            pltpu.VMEM((SAMPLES, WIDTH), BF16),
            pltpu.VMEM((WIDTH, SLICE), BF16),
            pltpu.VMEM((2, 4, 4, 8, 16, SLICE), BF16),
            pltpu.VMEM((8, LANES), F32),
            pltpu.VMEM((8, LANES), F32),
            pltpu.VMEM((128, *block), F32),
            pltpu.VMEM((8, WINDOW, *block), F32),
            pltpu.VMEM((8, 3, 4, *block), F32),
            pltpu.VMEM((2, 4, 4, *block), F32),
            pltpu.VMEM((2, 3, 4, *block), F32),
            pltpu.VMEM((8, *block), F32),
            pltpu.VMEM((7, *block), F32),
            pltpu.VMEM(tall, F32),
            pltpu.VMEM((15, 32, LANES), F32),
            pltpu.VMEM(tall, F32),
            pltpu.VMEM((15, 32, LANES), F32),
            pltpu.VMEM((WIDTH // 2, SLICE), F32),
            pltpu.VMEM((WIDTH // 2, SLICE), F32),
            pltpu.VMEM((WIDTH // 2, SLICE), BF16),
            pltpu.VMEM((8, 16, LANES), F32),
            pltpu.VMEM((7, 16, LANES), F32),
            pltpu.VMEM(block, F32),
            pltpu.VMEM(block, F32),
            pltpu.VMEM(block, F32),
            pltpu.VMEM(block, F32),
            dma((PARTS + 5,)),
            dma((8,)),
            dma((8,)),
            dma((8,)),
            dma((2,)),
            dma((8,)),
            dma((11,)),
        ],
        compiler_params=pltpu.CompilerParams(
            collective_id=0, has_side_effects=True, vmem_limit_bytes=63 * 1024 * 1024
        ),
        name="distill",
    )(client_counts, sample_ids, logits, student_hidden, student_weight, perm)
    grad_weight, turned = pl.pallas_call(
        finish,
        out_shape=(
            jax.ShapeDtypeStruct((WIDTH, SLICE), BF16),
            jax.ShapeDtypeStruct((16, SAMPLES), F32),
        ),
        in_specs=[vmem] * 3,
        out_specs=(any_spec, vmem),
        scratch_shapes=[pltpu.VMEM((WIDTH, SLICE), BF16), dma((4,))],
        compiler_params=pltpu.CompilerParams(vmem_limit_bytes=8 * 1024 * 1024),
        name="finish",
    )(grad, grad_hidden, student_hidden)
    return grad_weight, turned.T


def solution(mesh):
    both = ("hst", "local")
    return jax.shard_map(
        per_device,
        mesh=mesh,
        in_specs=(P(both, None, None), P(both, None), P(both), P(), P(None, both)),
        out_specs=(P(None, both), P(None, both)),
        check_vma=False,
    )
```

time: 214 us -> 45.4 us (0.21)
  waiting for transfers between devices: 69.4 us -> 0 us
  blocking collectives: 49 us -> 0 us
  Pallas kernels: 0 us -> 44.7 us
  starting transfers between devices: 42.7 us -> 0 us
  local copies, waits for them, and re-layouts: 31.9 us -> 0.01 us
  other arithmetic: 11.1 us -> 0 us
  matrix products: 8.22 us -> 0 us
    all_to_all x5 -> x0, waiting for transfers between devices: 69.4 us -> none  [the longest x1 35.4 us: sum_at_owner(): lax.all_to_all(blocks, axis, split_axis=0, concat_axis=0, tiled=True)]
    pallas_call x0 -> x2, Pallas kernels: none -> 44.7 us  [the longest x1 42.7 us: per_device(): pl.pallas_call(kernel, out_shape=(pltpu.VMEM((SAMPLES, SLICE), F32), pltp...]
    all_to_all x5 -> x0, starting transfers between devices: 42.7 us -> none  [the longest x2 19.1 us: sent_to_all(): lax.all_to_all(jnp.broadcast_to(shard[None], (devices, *shard.shape)), ax...]
    all_gather x4 -> x0, blocking collectives: 40.1 us -> none  [gathered_once(): both, at, found = (lax.all_gather(jnp.concatenate(lines), axis), 0, {})]
    reshape x5 -> x0, local copies, waits for them, and re-layouts: 16.7 us -> none  [cut_along(): shard.reshape(*lengths[:dim], devices, lengths[dim] // devices, *lengths[...]
    all_to_all x1 -> x0, blocking collectives: 8.87 us -> none  [sum_at_owner(): lax.all_to_all(blocks, axis, split_axis=0, concat_axis=0, tiled=True)]
    dot_general x5 -> x0, matrix products: 8.22 us -> none  [the longest x2 5.58 us: per_device(): jnp.dot(selector, teacher_logits[client], preferred_element_type=jnp.floa...]
    reduce_sum x9 -> x0, other arithmetic: 6.87 us -> none  [the longest x2 2.44 us: sum_at_owner(): return arrived.sum(axis=0)]
  transfers between devices with their start and end apart: 5 -> 0, of which waited for: 4 -> 0; matrix products, arithmetic and copies ran while one was open for 18% -> 0% of each run, Pallas kernels for 0% -> 0%
where the time goes in v2:
time: 45.4 us; the launch traced here: 45.3 us
  Pallas kernels  44.7 us (98%)
  between operations  0.65 us (1%)
    pallas_call x1, Pallas kernels, per_device(): pl.pallas_call(kernel, out_shape=(pltpu.VMEM((SAMPLES, SLICE), F32), pltp...  42.7 us
    pallas_call x1, Pallas kernels, per_device(): pl.pallas_call(finish, out_shape=(jax.ShapeDtypeStruct((WIDTH, SLICE), BF...  1.93 us

profile of v2, /device:TPU:1, one launch (start us, length us, event | category | flops | bytes accessed | tf_op | source)
XLA Modules:
  0.0 45.3 jit_solution(4774876260845156585)
XLA Ops:
  0.6 0.0 copy-start
  0.6 42.7 %distill.1 = (f32[24,125]{1,0:T(8,128)S(1)}, f32[24,16]{1,0:T(8,128)S(1)}) custom-call(s32[2]{0:T(128)} %counts_hbm.1, s32[2,24]{1,0:T(2,128)} %ids_hbm.1, bf16[48,32000]{1,0:T(8,128)(2,1)} %bitcast.4, bf16[24,4096]{1,0:T(8,128)(2,1)} %hidden.1, bf16[4096,125]{1,0:T(8,128)(2,1)} %weight_hbm.1, bf16[8,2,4,4,16,125]{5,4,3,2,1,0:T(8,128)(2,1)} %bitcast.3), custom_call_target="tpu_custom_call" | custom-call | tf_op jit(solution)/shard_map/distill/pallas_call | solution.py:439
  43.4 0.0 copy-done
  43.4 1.9 %finish.1 = (bf16[4096,125]{1,0:T(8,128)(2,1)}, f32[16,24]{1,0:T(8,128)}) custom-call(f32[24,125]{1,0:T(8,128)S(1)} %get-tuple-element.6.grad, f32[24,16]{1,0:T(8,128)S(1)} %get-tuple-element.7.grad_hidden, bf16[24,4096]{1,0:T(8,128)(2,1)S(1)} %copy-done), custom_call_target="tpu_custom_call" | custom-call | tf_op jit(solution)/shard_map/finish/pallas_call | solution.py:490
Async XLA Ops:
  0.6 42.7 %copy-start = (bf16[24,4096]{1,0:T(8,128)(2,1)S(1)}, bf16[24,4096]{1,0:T(8,128)(2,1)}, u32[]{:S(2)}) copy-start(bf16[24,4096]{1,0:T(8,128)(2,1)} %hidden.1) | copy-start | bytes 589828

commit v3 on v2

--- a/solution.py
+++ b/solution.py
@@ -20,7 +20,9 @@
 STEPS = tuple(-(-min(4000 * (k + 1) + LANES, VOCAB) // STEP_COLUMNS) for k in range(8))
 PARTS = 8
 WINDOW = 17
-LAG = 5
+LAG = 4
+DIRECT = 1
+ALONG_Z = 4 - DIRECT
 LOW = -3.0e38
 
 
@@ -119,10 +121,10 @@
     grad_ref, hidden_out,
     counts, ids, x_in, local, hidden, weight, w_perm,
     count_to, count_from, blocks, from_core,
-    got1, second, got2, third, from_z,
+    got1, second, got2, third, from_z, c_from, c_sum, c_got,
     t_own, t_plane, s_own, s_plane, w_to, w_from, w_other,
     z_to, z_from, teacher, student, s_other, t_other,
-    load_sems, core_recv, forward_recv, ring_recv, cross_recv, many_recv, send_sems,
+    load_sems, core_recv, ring_recv, cross_recv, many_recv, send_sems,
 ):
     hst, loc = lax.axis_index("hst"), lax.axis_index("local")
     z, c = hst // 2, hst % 2
@@ -143,7 +145,7 @@
             for k in range(PARTS)
         )
     ]
-    for load in early + loads:
+    for load in early + loads[:1]:
         load.start()
 
     barrier = pltpu.get_barrier_semaphore()
@@ -159,6 +161,8 @@
         greet(hst, ((y + k // 4) % 4) * 4 + (x + k % 4) % 4)
     greet(other, loc)
 
+    for load in loads[1:]:
+        load.start()
     late = [
         pltpu.make_async_copy(hidden_hbm, hidden, load_sems.at[PARTS + 2]),
         pltpu.make_async_copy(weight_hbm, weight, load_sems.at[PARTS + 3]),
@@ -228,11 +232,8 @@
     def arrived(ref, recv_sem):
         pltpu.make_async_copy(ref, ref, recv_sem).wait()
 
-    def pair(k, n, half):
-        return blocks.at[pl.ds(16 * k + 4 * n + 2 * half, 2)]
-
-    def landing(k, slot, half):
-        return got1.at[k, slot, pl.ds(2 * half, 2)]
+    def group(k, n, low=0, count=4):
+        return blocks.at[pl.ds(16 * k + 4 * n + low, count)]
 
     def receive_core(k):
         core_copies[k].wait_recv()
@@ -253,26 +254,23 @@
                         block = pltpu.roll(block, LANES - shift, 1)
                     blocks[16 * k + places[16 * (k % 2) + n]] = jnp.where(valid, block, counted)
 
+
+        @pl.when(z != k)
+        def along_z():
+            came_from = (k + 8 - z) % 8
+            send(
+                group(k, 2, DIRECT, ALONG_Z), c_from.at[came_from - 1], 11, many_recv.at[8],
+                2 * k + c, loc,
+            )
+
         way = ways[k % 2]
-        for half in range(2):
+        if DIRECT:
             send(
-                pair(k, 2, half), landing(k, 0, half), 1, forward_recv.at[k], hst,
-                way[3 if half else 1],
+                group(k, 2, 0, DIRECT), got1.at[k, pl.ds(8, DIRECT)], 1, ring_recv.at[k],
+                hst, way[2],
             )
-
-    def direct(k):
-        way = ways[k % 2]
-        send(pair(k, 1, 1), landing(k, 1, 1), 1, ring_recv.at[k], hst, way[1])
-        send(pair(k, 3, 0), landing(k, 2, 0), 1, ring_recv.at[k], hst, way[3])
-
-    def relay(k):
-        way = ways[k % 2]
-        arrived(got1.at[k, 0], forward_recv.at[k])
-        for half, near in ((0, 1), (1, 3)):
-            for n in range(2):
-                at = 16 * k + 4 * near + 2 * half + n
-                blocks[at] = blocks[at] + got1[k, 0, 2 * half + n]
-            send(pair(k, near, half), landing(k, 1 + half, half), 1, ring_recv.at[k], hst, way[near])
+        send(group(k, 1), got1.at[k, pl.ds(0, 4)], 1, ring_recv.at[k], hst, way[1])
+        send(group(k, 3), got1.at[k, pl.ds(4, 4)], 1, ring_recv.at[k], hst, way[3])
 
     for k in range(8):
         loads[k].wait()
@@ -293,20 +291,6 @@
             receive_core(k - LAG)
     for k in range(8 - LAG, 8):
         receive_core(k)
-    for k in range(8):
-        direct(k)
-    for k in range(8):
-        relay(k)
-    for k in range(8):
-        arrived(got1.at[k, pl.ds(1, 2)], ring_recv.at[k])
-        for n in range(4):
-            second[k % 2, n, k // 2] = blocks[16 * k + n] + (got1[k, 1, n] + got1[k, 2, n])
-    for n in (2, 1, 3):
-        for color in range(2):
-            send(
-                second.at[color, n], got2.at[color, n - 1], 2, cross_recv.at[color],
-                hst, ways[1 - color][n],
-            )
     for load in late:
         load.wait()
 
@@ -322,15 +306,6 @@
     student[:, :SLICE] = jnp.dot(hidden[...], weight[...], preferred_element_type=F32)
     student[:, SLICE:] = jnp.zeros((SAMPLES, LANES - SLICE), F32)
     s_copy = send(student, s_other, 7, many_recv.at[1], other, loc)
-    for color in range(2):
-        arrived(got2.at[color], cross_recv.at[color])
-        for item in range(4):
-            third[2 * item + color] = (second[color, 0, item] + got2[color, 0, item]) + (
-                got2[color, 1, item] + got2[color, 2, item]
-            )
-    for k in Z_FAR_FIRST:
-        to_z = (z + k) % 8
-        send(third.at[to_z], from_z.at[k - 1], 3, many_recv.at[2], to_z * 2 + c, loc)
     w_copy.wait_recv()
     w_other[...] = w_from[...].astype(BF16)
     s_copy.wait_recv()
@@ -338,6 +313,47 @@
     top, total = own_part(student[...], own_rows, s_own)
     other_part(top, total, s_other[...], w_other[...], s_own)
 
+    for half in range(2):
+        for k in range(4 * half, 4 * half + 4):
+            arrived(got1.at[k], ring_recv.at[k])
+            for n in range(4):
+                total = blocks[16 * k + n] + (got1[k, n] + got1[k, 4 + n])
+                if n < DIRECT:
+                    total = total + got1[k, 8 + n]
+                second[half, k % 2, n, k // 2 - 2 * half] = total
+        for n in (2, 1, 3):
+            for color in range(2):
+                send(
+                    second.at[half, color, n], got2.at[half, color, n - 1], 2,
+                    cross_recv.at[half], hst, ways[1 - color][n],
+                )
+    arrived(c_from, many_recv.at[8])
+    odd = z % 2
+    for n in range(ALONG_Z):
+        at = 16 * z + 8 + DIRECT + n
+        total = blocks[at]
+        for k in range(7):
+            total = total + c_from[k, n]
+        c_sum[n] = total
+        across = DIRECT + n
+        to_x = (x + 2 * (1 - odd) + across * odd) % 4
+        to_y = (y + 2 * odd + across * (1 - odd)) % 4
+        send(c_sum.at[n], c_got.at[n], 12, many_recv.at[9], hst, to_y * 4 + to_x)
+    for half in range(2):
+        arrived(got2.at[half], cross_recv.at[half])
+        for item in range(2):
+            for color in range(2):
+                to_z = 4 * half + 2 * item + color
+                third[to_z] = (second[half, color, 0, item] + got2[half, color, 0, item]) + (
+                    got2[half, color, 1, item] + got2[half, color, 2, item]
+                )
+        for to_z in range(4 * half, 4 * half + 4):
+
+            @pl.when(z != to_z)
+            def to_owner(to_z=to_z):
+                slot = (to_z + 8 - z) % 8 - 1
+                send(third.at[to_z], from_z.at[slot], 3, many_recv.at[2], 2 * to_z + c, loc)
+
     def plane(src, dst, sem, recv_sem):
         for k in FAR_FIRST:
             to = ((y + k // 4) % 4) * 4 + (x + k % 4) % 4
@@ -348,6 +364,9 @@
     summed = third[z]
     for k in range(7):
         summed = summed + from_z[k]
+    arrived(c_got, many_recv.at[9])
+    for n in range(ALONG_Z):
+        summed = summed + c_got[n]
 
     ensemble = summed / summed[:, SLICE : SLICE + 1]
     teacher[...] = ensemble
@@ -407,7 +426,7 @@
         grad_ref[rows, :] = (SCALE * (s_prob - t_prob))[:, :SLICE]
 
     for n, ref in enumerate(
-        (from_core, got1, got2, from_z, z_from, w_to, s_plane, student, t_plane, count_to, teacher)
+        (from_core, got1, got2, from_z, z_from, w_to, s_plane, student, t_plane, count_to, teacher, c_from, c_got)
     ):
         arrived(ref, send_sems.at[n])
 
@@ -456,11 +475,14 @@
             pltpu.VMEM((8, LANES), F32),
             pltpu.VMEM((128, *block), F32),
             pltpu.VMEM((8, WINDOW, *block), F32),
-            pltpu.VMEM((8, 3, 4, *block), F32),
-            pltpu.VMEM((2, 4, 4, *block), F32),
-            pltpu.VMEM((2, 3, 4, *block), F32),
+            pltpu.VMEM((8, 8 + DIRECT, *block), F32),
+            pltpu.VMEM((2, 2, 4, 2, *block), F32),
+            pltpu.VMEM((2, 2, 3, 2, *block), F32),
             pltpu.VMEM((8, *block), F32),
             pltpu.VMEM((7, *block), F32),
+            pltpu.VMEM((7, ALONG_Z, *block), F32),
+            pltpu.VMEM((ALONG_Z, *block), F32),
+            pltpu.VMEM((ALONG_Z, *block), F32),
             pltpu.VMEM(tall, F32),
             pltpu.VMEM((15, 32, LANES), F32),
             pltpu.VMEM(tall, F32),
@@ -477,10 +499,9 @@
             dma((PARTS + 5,)),
             dma((8,)),
             dma((8,)),
-            dma((8,)),
             dma((2,)),
-            dma((8,)),
-            dma((11,)),
+            dma((10,)),
+            dma((13,)),
         ],
         compiler_params=pltpu.CompilerParams(
             collective_id=0, has_side_effects=True, vmem_limit_bytes=63 * 1024 * 1024

time: 45.4 us -> 43.9 us (0.967)
  Pallas kernels: 44.7 us -> 43.1 us
    pallas_call x1, Pallas kernels: 42.7 us -> 41.2 us  [per_device(): pl.pallas_call(kernel, out_shape=(pltpu.VMEM((SAMPLES, SLICE), F32), pltp...]
where the time goes in v3:
time: 43.9 us; the launch traced here: 43.8 us
  Pallas kernels  43.1 us (98%)
  between operations  0.65 us (1%)
    pallas_call x1, Pallas kernels, per_device(): pl.pallas_call(kernel, out_shape=(pltpu.VMEM((SAMPLES, SLICE), F32), pltp...  41.2 us
    pallas_call x1, Pallas kernels, per_device(): pl.pallas_call(finish, out_shape=(jax.ShapeDtypeStruct((WIDTH, SLICE), BF...  1.93 us

profile of v3, /device:TPU:1, one launch (start us, length us, event | category | flops | bytes accessed | tf_op | source)
XLA Modules:
  0.0 43.8 jit_solution(16702359656731966546)
XLA Ops:
  0.6 0.0 copy-start
  0.6 41.2 %distill.1 = (f32[24,125]{1,0:T(8,128)S(1)}, f32[24,16]{1,0:T(8,128)S(1)}) custom-call(s32[2]{0:T(128)} %counts_hbm.1, s32[2,24]{1,0:T(2,128)} %ids_hbm.1, bf16[48,32000]{1,0:T(8,128)(2,1)} %bitcast.4, bf16[24,4096]{1,0:T(8,128)(2,1)} %hidden.1, bf16[4096,125]{1,0:T(8,128)(2,1)} %weight_hbm.1, bf16[8,2,4,4,16,125]{5,4,3,2,1,0:T(8,128)(2,1)} %bitcast.3), custom_call_target="tpu_custom_call" | custom-call | tf_op jit(solution)/shard_map/distill/pallas_call | solution.py:458
  41.8 0.0 copy-done
  41.9 1.9 %finish.1 = (bf16[4096,125]{1,0:T(8,128)(2,1)}, f32[16,24]{1,0:T(8,128)}) custom-call(f32[24,125]{1,0:T(8,128)S(1)} %get-tuple-element.6.grad, f32[24,16]{1,0:T(8,128)S(1)} %get-tuple-element.7.grad_hidden, bf16[24,4096]{1,0:T(8,128)(2,1)S(1)} %copy-done), custom_call_target="tpu_custom_call" | custom-call | tf_op jit(solution)/shard_map/finish/pallas_call | solution.py:511
Async XLA Ops:
  0.6 41.2 %copy-start = (bf16[24,4096]{1,0:T(8,128)(2,1)S(1)}, bf16[24,4096]{1,0:T(8,128)(2,1)}, u32[]{:S(2)}) copy-start(bf16[24,4096]{1,0:T(8,128)(2,1)} %hidden.1) | copy-start | bytes 589828

commit v4 on v3

--- a/solution.py
+++ b/solution.py
@@ -21,6 +21,7 @@
 PARTS = 8
 WINDOW = 17
 LAG = 4
+ITEMS = ((0, 2), (2, 1), (3, 1))
 DIRECT = 1
 ALONG_Z = 4 - DIRECT
 LOW = -3.0e38
@@ -313,19 +314,20 @@
     top, total = own_part(student[...], own_rows, s_own)
     other_part(top, total, s_other[...], w_other[...], s_own)
 
-    for half in range(2):
-        for k in range(4 * half, 4 * half + 4):
+    for part, (first_item, items) in enumerate(ITEMS):
+        for k in range(2 * first_item, 2 * (first_item + items)):
             arrived(got1.at[k], ring_recv.at[k])
             for n in range(4):
                 total = blocks[16 * k + n] + (got1[k, n] + got1[k, 4 + n])
                 if n < DIRECT:
                     total = total + got1[k, 8 + n]
-                second[half, k % 2, n, k // 2 - 2 * half] = total
+                second[k % 2, n, k // 2] = total
+        taken = pl.ds(first_item, items)
         for n in (2, 1, 3):
             for color in range(2):
                 send(
-                    second.at[half, color, n], got2.at[half, color, n - 1], 2,
-                    cross_recv.at[half], hst, ways[1 - color][n],
+                    second.at[color, n, taken], got2.at[color, n - 1, taken], 2,
+                    cross_recv.at[part], hst, ways[1 - color][n],
                 )
     arrived(c_from, many_recv.at[8])
     odd = z % 2
@@ -339,15 +341,15 @@
         to_x = (x + 2 * (1 - odd) + across * odd) % 4
         to_y = (y + 2 * odd + across * (1 - odd)) % 4
         send(c_sum.at[n], c_got.at[n], 12, many_recv.at[9], hst, to_y * 4 + to_x)
-    for half in range(2):
-        arrived(got2.at[half], cross_recv.at[half])
-        for item in range(2):
+    for part, (first_item, items) in enumerate(ITEMS):
+        arrived(got2.at[:, :, pl.ds(first_item, items)], cross_recv.at[part])
+        for item in range(first_item, first_item + items):
             for color in range(2):
-                to_z = 4 * half + 2 * item + color
-                third[to_z] = (second[half, color, 0, item] + got2[half, color, 0, item]) + (
-                    got2[half, color, 1, item] + got2[half, color, 2, item]
+                third[2 * item + color] = (second[color, 0, item] + got2[color, 0, item]) + (
+                    got2[color, 1, item] + got2[color, 2, item]
                 )
-        for to_z in range(4 * half, 4 * half + 4):
+        for n in range(2 * items):
+            to_z = 2 * first_item + (z + 1 + n) % (2 * items)
 
             @pl.when(z != to_z)
             def to_owner(to_z=to_z):
@@ -476,8 +478,8 @@
             pltpu.VMEM((128, *block), F32),
             pltpu.VMEM((8, WINDOW, *block), F32),
             pltpu.VMEM((8, 8 + DIRECT, *block), F32),
-            pltpu.VMEM((2, 2, 4, 2, *block), F32),
-            pltpu.VMEM((2, 2, 3, 2, *block), F32),
+            pltpu.VMEM((2, 4, 4, *block), F32),
+            pltpu.VMEM((2, 3, 4, *block), F32),
             pltpu.VMEM((8, *block), F32),
             pltpu.VMEM((7, *block), F32),
             pltpu.VMEM((7, ALONG_Z, *block), F32),
@@ -499,7 +501,7 @@
             dma((PARTS + 5,)),
             dma((8,)),
             dma((8,)),
-            dma((2,)),
+            dma((3,)),
             dma((10,)),
             dma((13,)),
         ],

time: 43.9 us -> 43.1 us (0.982)
  Pallas kernels: 43.1 us -> 42.4 us
    pallas_call x1, Pallas kernels: 41.2 us -> 40.4 us  [per_device(): pl.pallas_call(kernel, out_shape=(pltpu.VMEM((SAMPLES, SLICE), F32), pltp...]
where the time goes in v4:
time: 43.1 us; the launch traced here: 43 us
  Pallas kernels  42.4 us (98%)
  between operations  0.65 us (2%)
    pallas_call x1, Pallas kernels, per_device(): pl.pallas_call(kernel, out_shape=(pltpu.VMEM((SAMPLES, SLICE), F32), pltp...  40.4 us
    pallas_call x1, Pallas kernels, per_device(): pl.pallas_call(finish, out_shape=(jax.ShapeDtypeStruct((WIDTH, SLICE), BF...  1.93 us

profile of v4, /device:TPU:1, one launch (start us, length us, event | category | flops | bytes accessed | tf_op | source)
XLA Modules:
  0.0 43.0 jit_solution(14049599953677564161)
XLA Ops:
  0.6 0.0 copy-start
  0.6 40.4 %distill.1 = (f32[24,125]{1,0:T(8,128)S(1)}, f32[24,16]{1,0:T(8,128)S(1)}) custom-call(s32[2]{0:T(128)} %counts_hbm.1, s32[2,24]{1,0:T(2,128)} %ids_hbm.1, bf16[48,32000]{1,0:T(8,128)(2,1)} %bitcast.4, bf16[24,4096]{1,0:T(8,128)(2,1)} %hidden.1, bf16[4096,125]{1,0:T(8,128)(2,1)} %weight_hbm.1, bf16[8,2,4,4,16,125]{5,4,3,2,1,0:T(8,128)(2,1)} %bitcast.3), custom_call_target="tpu_custom_call" | custom-call | tf_op jit(solution)/shard_map/distill/pallas_call | solution.py:460
  41.1 0.0 copy-done
  41.1 1.9 %finish.1 = (bf16[4096,125]{1,0:T(8,128)(2,1)}, f32[16,24]{1,0:T(8,128)}) custom-call(f32[24,125]{1,0:T(8,128)S(1)} %get-tuple-element.6.grad, f32[24,16]{1,0:T(8,128)S(1)} %get-tuple-element.7.grad_hidden, bf16[24,4096]{1,0:T(8,128)(2,1)S(1)} %copy-done), custom_call_target="tpu_custom_call" | custom-call | tf_op jit(solution)/shard_map/finish/pallas_call | solution.py:513
Async XLA Ops:
  0.6 40.5 %copy-start = (bf16[24,4096]{1,0:T(8,128)(2,1)S(1)}, bf16[24,4096]{1,0:T(8,128)(2,1)}, u32[]{:S(2)}) copy-start(bf16[24,4096]{1,0:T(8,128)(2,1)} %hidden.1) | copy-start | bytes 589828

commit v5 on v4

--- a/solution.py
+++ b/solution.py
@@ -15,6 +15,7 @@
 LANES = 128
 SCALE = 32768.0 / SAMPLES
 Z_FAR_FIRST = (4, 3, 5, 2, 6, 1, 7)
+NEIGHBOURS = (2, 1, 3, 0)
 FAR_FIRST = (10, 6, 9, 11, 14, 2, 8, 5, 7, 13, 15, 1, 3, 4, 12)
 STEP_COLUMNS = 512
 STEPS = tuple(-(-min(4000 * (k + 1) + LANES, VOCAB) // STEP_COLUMNS) for k in range(8))
@@ -48,13 +49,17 @@
     )
 
 
-def weighted_product(values, top, rows):
+def masked_weights(values, top):
     valid = lane_index(SAMPLES) < SLICE
     weights = jnp.where(valid, jnp.exp(values - top), 0.0)
+    return split_two(weights), jnp.sum(weights, axis=1, keepdims=True)
+
+
+def product_with(weights, rows):
     product = lax.dot_general(
-        split_two(weights), rows, (((1,), (1,)), ((), ())), preferred_element_type=F32
+        weights, rows, (((1,), (1,)), ((), ())), preferred_element_type=F32
     )
-    return jnp.sum(weights, axis=1, keepdims=True), product[:SAMPLES] + product[SAMPLES:]
+    return product[:SAMPLES] + product[SAMPLES:]
 
 
 def packed_stats(top, total):
@@ -75,22 +80,30 @@
 
 def own_part(own, rows, out):
     top = masked_top(own)
-    total, product = weighted_product(own, top, rows)
+    weights, total = masked_weights(own, top)
+    product = product_with(weights, rows)
     for b in range(16):
         out[b, 0:SAMPLES, :] = product[:, LANES * b : LANES * (b + 1)]
     return top, total
 
 
-def other_part(top, total, other, rows, out):
+def other_part(top, total, other, rows, out, y, finished):
     joined = jnp.maximum(top, masked_top(other))
-    more, product = weighted_product(other, joined, rows)
+    weights, more = masked_weights(other, joined)
     scale = jnp.exp(top - joined)
     stats = packed_stats(joined, total * scale + more)
-    for b in range(16):
-        out[b, 0:SAMPLES, :] = (
-            out[b, 0:SAMPLES, :] * scale + product[:, LANES * b : LANES * (b + 1)]
+    for dy in NEIGHBOURS:
+        to_y = (y + dy) % 4
+        product = product_with(
+            weights, rows[pl.ds(pl.multiple_of(to_y * 4 * LANES, 4 * LANES), 4 * LANES), :]
         )
-        out[b, SAMPLES:32, :] = stats
+        for n in range(4):
+            b = 4 * to_y + n
+            out[b, 0:SAMPLES, :] = (
+                out[b, 0:SAMPLES, :] * scale + product[:, LANES * n : LANES * (n + 1)]
+            )
+            out[b, SAMPLES:32, :] = stats
+        finished(dy, to_y)
 
 
 def factors(stat, joined):
@@ -267,11 +280,11 @@
         way = ways[k % 2]
         if DIRECT:
             send(
-                group(k, 2, 0, DIRECT), got1.at[k, pl.ds(8, DIRECT)], 1, ring_recv.at[k],
+                group(k, 2, 0, DIRECT), got1.at[k, pl.ds(8, DIRECT)], 1, ring_recv.at[max(0, k // 2 - 1)],
                 hst, way[2],
             )
-        send(group(k, 1), got1.at[k, pl.ds(0, 4)], 1, ring_recv.at[k], hst, way[1])
-        send(group(k, 3), got1.at[k, pl.ds(4, 4)], 1, ring_recv.at[k], hst, way[3])
+        send(group(k, 1), got1.at[k, pl.ds(0, 4)], 1, ring_recv.at[max(0, k // 2 - 1)], hst, way[1])
+        send(group(k, 3), got1.at[k, pl.ds(4, 4)], 1, ring_recv.at[max(0, k // 2 - 1)], hst, way[3])
 
     for k in range(8):
         loads[k].wait()
@@ -312,11 +325,11 @@
     s_copy.wait_recv()
     own_rows = w_perm[c].reshape(WIDTH // 2, SLICE)
     top, total = own_part(student[...], own_rows, s_own)
-    other_part(top, total, s_other[...], w_other[...], s_own)
+    other_part(top, total, s_other[...], w_other, s_own, y, lambda dy, to_y: None)
 
     for part, (first_item, items) in enumerate(ITEMS):
+        arrived(got1.at[pl.ds(2 * first_item, 2 * items)], ring_recv.at[part])
         for k in range(2 * first_item, 2 * (first_item + items)):
-            arrived(got1.at[k], ring_recv.at[k])
             for n in range(4):
                 total = blocks[16 * k + n] + (got1[k, n] + got1[k, 4 + n])
                 if n < DIRECT:
@@ -375,9 +388,14 @@
     t_copy = send(teacher, t_other, 10, many_recv.at[7], other, loc)
     top, total = own_part(ensemble, own_rows, t_own)
     t_copy.wait_recv()
-    other_part(top, total, t_other[...], w_other[...], t_own)
-    plane(t_own, t_plane, 8, many_recv.at[4])
-
+    def send_row(dy, to_y):
+        for dx in NEIGHBOURS:
+            k = 4 * dy + dx
+            if k:
+                to = to_y * 4 + (x + dx) % 4
+                send(t_own.at[to], t_plane.at[k - 1], 8, many_recv.at[4], hst, to)
+
+    other_part(top, total, t_other[...], w_other, t_own, y, send_row)
     arrived(s_plane, many_recv.at[3])
     s_sums, s_tops, s_totals = join_plane(s_own, loc, s_plane)
     lane8 = lane_index(8)
@@ -500,7 +518,7 @@
             pltpu.VMEM(block, F32),
             dma((PARTS + 5,)),
             dma((8,)),
-            dma((8,)),
+            dma((3,)),
             dma((3,)),
             dma((10,)),
             dma((13,)),

time: 43.1 us -> 42.6 us (0.988)
  Pallas kernels: 42.4 us -> 41.8 us
    pallas_call x1, Pallas kernels: 40.4 us -> 39.9 us  [per_device(): pl.pallas_call(kernel, out_shape=(pltpu.VMEM((SAMPLES, SLICE), F32), pltp...]
where the time goes in v5:
time: 42.6 us; the launch traced here: 42.5 us
  Pallas kernels  41.8 us (98%)
  between operations  0.65 us (2%)
    pallas_call x1, Pallas kernels, per_device(): pl.pallas_call(kernel, out_shape=(pltpu.VMEM((SAMPLES, SLICE), F32), pltp...  39.9 us
    pallas_call x1, Pallas kernels, per_device(): pl.pallas_call(finish, out_shape=(jax.ShapeDtypeStruct((WIDTH, SLICE), BF...  1.93 us

profile of v5, /device:TPU:1, one launch (start us, length us, event | category | flops | bytes accessed | tf_op | source)
XLA Modules:
  0.0 42.5 jit_solution(15814573761660709033)
XLA Ops:
  0.6 0.0 copy-start
  0.6 39.9 %distill.1 = (f32[24,125]{1,0:T(8,128)S(1)}, f32[24,16]{1,0:T(8,128)S(1)}) custom-call(s32[2]{0:T(128)} %counts_hbm.1, s32[2,24]{1,0:T(2,128)} %ids_hbm.1, bf16[48,32000]{1,0:T(8,128)(2,1)} %bitcast.4, bf16[24,4096]{1,0:T(8,128)(2,1)} %hidden.1, bf16[4096,125]{1,0:T(8,128)(2,1)} %weight_hbm.1, bf16[8,2,4,4,16,125]{5,4,3,2,1,0:T(8,128)(2,1)} %bitcast.3), custom_call_target="tpu_custom_call" | custom-call | tf_op jit(solution)/shard_map/distill/pallas_call | solution.py:478
  40.5 0.0 copy-done
  40.5 1.9 %finish.1 = (bf16[4096,125]{1,0:T(8,128)(2,1)}, f32[16,24]{1,0:T(8,128)}) custom-call(f32[24,125]{1,0:T(8,128)S(1)} %get-tuple-element.6.grad, f32[24,16]{1,0:T(8,128)S(1)} %get-tuple-element.7.grad_hidden, bf16[24,4096]{1,0:T(8,128)(2,1)S(1)} %copy-done), custom_call_target="tpu_custom_call" | custom-call | tf_op jit(solution)/shard_map/finish/pallas_call | solution.py:531
Async XLA Ops:
  0.6 39.9 %copy-start = (bf16[24,4096]{1,0:T(8,128)(2,1)S(1)}, bf16[24,4096]{1,0:T(8,128)(2,1)}, u32[]{:S(2)}) copy-start(bf16[24,4096]{1,0:T(8,128)(2,1)} %hidden.1) | copy-start | bytes 589828

commit v6 on v5

--- a/solution.py
+++ b/solution.py
@@ -342,19 +342,23 @@
                     second.at[color, n, taken], got2.at[color, n - 1, taken], 2,
                     cross_recv.at[part], hst, ways[1 - color][n],
                 )
-    arrived(c_from, many_recv.at[8])
-    odd = z % 2
-    for n in range(ALONG_Z):
-        at = 16 * z + 8 + DIRECT + n
-        total = blocks[at]
-        for k in range(7):
-            total = total + c_from[k, n]
-        c_sum[n] = total
-        across = DIRECT + n
-        to_x = (x + 2 * (1 - odd) + across * odd) % 4
-        to_y = (y + 2 * odd + across * (1 - odd)) % 4
-        send(c_sum.at[n], c_got.at[n], 12, many_recv.at[9], hst, to_y * 4 + to_x)
+    def sum_far_blocks():
+        arrived(c_from, many_recv.at[8])
+        odd = z % 2
+        for n in range(ALONG_Z):
+            at = 16 * z + 8 + DIRECT + n
+            total = blocks[at]
+            for k in range(7):
+                total = total + c_from[k, n]
+            c_sum[n] = total
+            across = DIRECT + n
+            to_x = (x + 2 * (1 - odd) + across * odd) % 4
+            to_y = (y + 2 * odd + across * (1 - odd)) % 4
+            send(c_sum.at[n], c_got.at[n], 12, many_recv.at[9], hst, to_y * 4 + to_x)
+
     for part, (first_item, items) in enumerate(ITEMS):
+        if part == 2:
+            sum_far_blocks()
         arrived(got2.at[:, :, pl.ds(first_item, items)], cross_recv.at[part])
         for item in range(first_item, first_item + items):
             for color in range(2):

time: 42.6 us -> 42.3 us (level)
  no operation moved by 1% of the time
where the time goes in v6:
time: 42.3 us; the launch traced here: 42.2 us
  Pallas kernels  41.6 us (98%)
  between operations  0.65 us (2%)
    pallas_call x1, Pallas kernels, per_device(): pl.pallas_call(kernel, out_shape=(pltpu.VMEM((SAMPLES, SLICE), F32), pltp...  39.6 us
    pallas_call x1, Pallas kernels, per_device(): pl.pallas_call(finish, out_shape=(jax.ShapeDtypeStruct((WIDTH, SLICE), BF...  1.94 us

profile of v6, /device:TPU:1, one launch (start us, length us, event | category | flops | bytes accessed | tf_op | source)
XLA Modules:
  0.0 42.2 jit_solution(11144673910111299273)
XLA Ops:
  0.6 0.0 copy-start
  0.6 39.6 %distill.1 = (f32[24,125]{1,0:T(8,128)S(1)}, f32[24,16]{1,0:T(8,128)S(1)}) custom-call(s32[2]{0:T(128)} %counts_hbm.1, s32[2,24]{1,0:T(2,128)} %ids_hbm.1, bf16[48,32000]{1,0:T(8,128)(2,1)} %bitcast.4, bf16[24,4096]{1,0:T(8,128)(2,1)} %hidden.1, bf16[4096,125]{1,0:T(8,128)(2,1)} %weight_hbm.1, bf16[8,2,4,4,16,125]{5,4,3,2,1,0:T(8,128)(2,1)} %bitcast.3), custom_call_target="tpu_custom_call" | custom-call | tf_op jit(solution)/shard_map/distill/pallas_call | solution.py:482
  40.3 0.0 copy-done
  40.3 1.9 %finish.1 = (bf16[4096,125]{1,0:T(8,128)(2,1)}, f32[16,24]{1,0:T(8,128)}) custom-call(f32[24,125]{1,0:T(8,128)S(1)} %get-tuple-element.6.grad, f32[24,16]{1,0:T(8,128)S(1)} %get-tuple-element.7.grad_hidden, bf16[24,4096]{1,0:T(8,128)(2,1)S(1)} %copy-done), custom_call_target="tpu_custom_call" | custom-call | tf_op jit(solution)/shard_map/finish/pallas_call | solution.py:535
Async XLA Ops:
  0.6 39.7 %copy-start = (bf16[24,4096]{1,0:T(8,128)(2,1)S(1)}, bf16[24,4096]{1,0:T(8,128)(2,1)}, u32[]{:S(2)}) copy-start(bf16[24,4096]{1,0:T(8,128)(2,1)} %hidden.1) | copy-start | bytes 589828
